TPU v7x, 32 devices: a whole 2x2x4 slice. The times are simulated.
32 devices in a mesh: seq: 16 (over z, y, x), head: 2 (over core).
Axes of the slice: x: 2, y: 2, z: 4, core: 2. Of those that a mesh axis runs over, the one named last changes fastest.
Arguments:
- queries: bfloat16 [3072, 32, 128], P('seq', 'head'), may hold values from -180 to 180
- key_rows: bfloat16 [3072, 8, 128], P('seq', 'head'), may hold values from -4.5 to 4.5
- value_rows: bfloat16 [3072, 8, 128], P('seq', 'head'), may hold values from -24 to 24
- windows: int32 [32], P('head'), may hold values from 768 to 1536, as said below
- sink_counts: int32 [32], P('head'), may hold values from 1 to 4, as said below
- sink_bias: float32 [32], P('head'), may hold values from 3 to 7
- out_weight: bfloat16 [4096, 4096], P('head'), may hold values from -0.09375 to 0.09375
Outputs:
- attn_out: bfloat16 [3072, 4096], P(('seq', 'head'))
Inputs may be any that keep to these rules, and one draw needn't show every extreme that they name: `windows`: each head's window lies between 768 and 1536, and some head has exactly 1536. `sink_counts`: each head has 1 to 4 sink tokens, and some head has exactly 4.
All inputs are finite; a program needn't handle non-finite values.
Results may differ from a plain program's by a relative error of at most 0.018.
Values may be sent and summed in bfloat16 or wider, within the bound.
A program may use at most 128 MiB of HBM per device.

v0:
```python
import functools

import jax
import jax.numpy as jnp
from jax import lax
from jax.experimental import pallas as pl
from jax.experimental.pallas import tpu as pltpu
from jax.sharding import PartitionSpec as P

WINDOW = 1536
SINKS = 4
PLANE = 4
SINK_ROWS = 16
HIDDEN = -1e30
LOG2E = 1.4426950408889634
MESH = pl.DeviceIdType.MESH


def kernel(
    n_seq, n_head, tile,
    win_ref, cnt_ref, bias_ref, k_hbm, v_hbm, q_hbm, w_hbm, out_ref,
    own, q_ref, kv, sink, qt, low, few, lift, top, norm, acc, att, w, part, got,
    send_sem, recv_sem, sink_send, sink_recv, own_sem, q_sem, w_sem, part_send, part_recv,
):
    me, side = lax.axis_index("seq"), lax.axis_index("head")
    heads_kv, _, rows, width = own.shape
    lanes = q_ref.shape[1]
    group = lanes // rows
    model = w.shape[1]
    share = rows // n_head
    z, p = me // PLANE, lax.rem(me, PLANE)
    bit0, bit1 = lax.rem(p, 2), p // 2
    px, py = p + 1 - 2 * bit0, p + 2 - 4 * bit1
    pd = 3 - p
    base = z * PLANE
    n_z = n_seq // PLANE
    scale = LOG2E / width**0.5

    barrier = pltpu.get_barrier_semaphore()

    def greet(where):
        pl.semaphore_signal(barrier, inc=1, device_id=where, device_id_type=MESH)

    above, below = (z + 1 < n_z).astype(jnp.int32), (z > 0).astype(jnp.int32)
    loads = [
        pltpu.make_async_copy(ref.at[c], own.at[c, k], own_sem.at[c, k])
        for c in range(heads_kv) for k, ref in enumerate((k_hbm, v_hbm))
    ]
    for load in loads:
        load.start()
    q_load = pltpu.make_async_copy(q_hbm, q_ref, q_sem)
    q_load.start()
    greet({"seq": base + px})
    greet({"seq": base + py})

    @pl.when(z + 1 < n_z)
    def _():
        greet({"seq": me + PLANE})

    @pl.when(z > 0)
    def _():
        greet({"seq": me - PLANE})

    for step in range(1, n_head):
        greet({"head": lax.rem(side + step, n_head)})
    pl.semaphore_wait(barrier, n_head + 1 + above + below)

    def send(kind, src, plane, source, c, target):
        return pltpu.make_async_remote_copy(
            src_ref=src,
            dst_ref=kv.at[plane * PLANE + source, c],
            send_sem=send_sem.at[kind, c],
            recv_sem=recv_sem.at[plane * PLANE + source, c],
            device_id={"seq": target},
            device_id_type=MESH,
        )

    def landed(plane, source, c):
        send(0, own.at[c], plane, source, c, me).wait_recv()

    def held(plane, source, c):
        return kv.at[plane * PLANE + source, c]

    x_old, y_old, d_old = 2 * bit0, 2 * bit1, 2 * bit1
    x_from, y_from, d_from = 2 - 2 * bit0, 2 - 2 * bit1, 2 - 2 * bit1

    def sink_copy(way, source, target):
        return pltpu.make_async_remote_copy(
            src_ref=source,
            dst_ref=sink,
            send_sem=sink_send.at[way],
            recv_sem=sink_recv,
            device_id={"seq": target},
            device_id_type=MESH,
        )

    first_rows = own.at[:, :, pl.ds(0, SINK_ROWS)]

    for load in loads:
        load.wait()
    for c in range(heads_kv):
        @pl.when(z + 1 < n_z)
        def _():
            send(0, own.at[c], 1, p, c, me + PLANE).start()

        @pl.when(x_old == 0)
        def _():
            send(2, own.at[c], 0, p, c, base + px).start()

        @pl.when(y_old == 0)
        def _():
            send(3, own.at[c], 0, p, c, base + py).start()

        if c == 0:
            @pl.when(me == 0)
            def _():
                sink_copy(0, first_rows, base + px).start()
                sink_copy(1, first_rows, base + py).start()

                @pl.when(z + 1 < n_z)
                def _():
                    sink_copy(2, first_rows, me + PLANE).start()

    fetch = pltpu.make_async_copy(w_hbm, w, w_sem)
    fetch.start()

    q_load.wait()
    column = lax.broadcasted_iota(jnp.int32, (1, lanes), 1)
    for c in range(heads_kv):
        window, count, bias, token = (jnp.zeros((1, lanes), t) for t in (jnp.int32, jnp.int32, jnp.float32, jnp.int32))
        for g in range(group):
            mine = (column >= g * rows) & (column < (g + 1) * rows)
            h = c * group + g
            window = jnp.where(mine, win_ref[h], window)
            count = jnp.where(mine, cnt_ref[h], count)
            bias = jnp.where(mine, bias_ref[h], bias)
            token = jnp.where(mine, column - g * rows, token)
        token = token + me * rows
        low[c] = jnp.maximum(token - window, count - 1)
        few[c] = jnp.minimum(token, count - 1)
        lift[c] = bias * LOG2E
        qt[c] = q_ref[c].T
        top[c] = jnp.full((1, lanes), HIDDEN, jnp.float32)
        norm[c] = jnp.zeros((1, lanes), jnp.float32)
        acc[c] = jnp.zeros((width, lanes), jnp.float32)

    def attend(block, c, shard, causal=False, sinks=False):
        keys, values = block[0], block[1]
        key_row = lax.broadcasted_iota(jnp.int32, (keys.shape[0], 1), 0)
        step = min(256, lanes)
        parts = [slice(n, n + step) for n in range(0, lanes, step)]
        scores = [jnp.dot(keys, qt[c, :, cols], preferred_element_type=jnp.float32) for cols in parts]
        turned = values.T
        olds = [top[c, :, cols] for cols in parts]
        weights, news, fades, sums = [], [], [], []
        for s, old, cols in zip(scores, olds, parts):
            s = s * scale
            if sinks:
                s = jnp.where(key_row <= few[c, :, cols], s + lift[c, :, cols], HIDDEN)
            else:
                seen = key_row > low[c, :, cols] - shard * rows
                if causal:
                    column = lax.broadcasted_iota(jnp.int32, (1, step), 1) + cols.start
                    seen = seen & (key_row <= lax.rem(column, rows))
                s = jnp.where(seen, s, HIDDEN)
            new = jnp.maximum(old, jnp.max(s, axis=0, keepdims=True))
            e = jnp.exp2(s - new)
            weights.append(e.astype(jnp.bfloat16))
            news.append(new)
            fades.append(jnp.exp2(old - new))
            sums.append(jnp.sum(e, axis=0, keepdims=True))
        adds = [jnp.dot(turned, e, preferred_element_type=jnp.float32) for e in weights]
        for new, fade, total, add, cols in zip(news, fades, sums, adds, parts):
            top[c, :, cols] = new
            norm[c, :, cols] = norm[c, :, cols] * fade + total
            acc[c, :, cols] = acc[c, :, cols] * fade + add

    def each(body):
        def one(c, carry):
            body(c)
            return carry
        lax.fori_loop(0, heads_kv, one, 0)

    each(lambda c: attend(own.at[c], c, me, causal=True))

    @pl.when(z >= 1)
    def _():
        def first(c):
            landed(1, p, c)

            @pl.when(z + 1 < n_z)
            def _():
                send(1, held(1, p, c), 2, p, c, me + PLANE).start()

            send(4, held(1, p, c), 1, p, c, base + px).start()
            send(5, held(1, p, c), 1, p, c, base + py).start()
            attend(held(1, p, c), c, me - PLANE)
        each(first)

    def pass_on():
        sink_copy(0, sink, me).wait_recv()

        @pl.when(me == 1)
        def _():
            sink_copy(1, sink, base + py).start()

        @pl.when(z + 1 < n_z)
        def _():
            sink_copy(2, sink, me + PLANE).start()

    @pl.when((me > 0) & (z <= 1))
    def _():
        pass_on()

    @pl.when(z >= 1)
    def _():
        def second(c):
            @pl.when(z >= 2)
            def _():
                landed(2, p, c)

                @pl.when(x_old == 2)
                def _():
                    send(2, held(2, p, c), 2, p, c, base + px).start()

                @pl.when(y_old == 2)
                def _():
                    send(3, held(2, p, c), 2, p, c, base + py).start()

            landed(1, px, c)
            send(6, held(1, px, c), 1, px, c, base + py).start()
            attend(held(1, px, c), c, base - PLANE + px)
        each(second)

    def relay(c):
        @pl.when(z >= y_from)
        def _():
            landed(y_from, py, c)
            send(7, held(y_from, py, c), y_from, py, c, base + px).start()
            attend(held(y_from, py, c), c, base - y_from * PLANE + py)
    each(relay)

    @pl.when(z >= 2)
    def _():
        pass_on()

    @pl.when(me == 0)
    def _():
        each(lambda c: attend(own.at[c, :, pl.ds(0, SINK_ROWS)], c, 0, sinks=True))

    @pl.when(me > 0)
    def _():
        each(lambda c: attend(sink.at[c], c, 0, sinks=True))

    @pl.when(z >= 2)
    def _():
        each(lambda c: attend(held(2, p, c), c, me - 2 * PLANE))

    @pl.when(z >= 1)
    def _():
        def third(c):
            landed(1, py, c)
            attend(held(1, py, c), c, base - PLANE + py)
        each(third)

    @pl.when(z >= x_from)
    def _():
        def fourth(c):
            landed(x_from, px, c)
            attend(held(x_from, px, c), c, base - x_from * PLANE + px)
        each(fourth)

    @pl.when(z >= 1)
    def _():
        def fifth(c):
            landed(1, pd, c)
            attend(held(1, pd, c), c, base - PLANE + pd)
        each(fifth)

    @pl.when(z >= d_from)
    def _():
        def sixth(c):
            landed(d_from, pd, c)
            attend(held(d_from, pd, c), c, base - d_from * PLANE + pd)
        each(sixth)

    for c in range(heads_kv):
        mixed = (acc[c] / norm[c]).T.astype(jnp.bfloat16)
        for g in range(group):
            h = c * group + g
            att[:, h * width:(h + 1) * width] = mixed[g * rows:(g + 1) * rows]

    fetch.wait()
    tiles = model // tile

    def give(t, step):
        target = lax.rem(side + step, n_head)
        return pltpu.make_async_remote_copy(
            src_ref=part.at[t, target],
            dst_ref=got.at[t, step - 1],
            send_sem=part_send.at[t, step - 1],
            recv_sem=part_recv.at[t, step - 1],
            device_id={"head": target},
            device_id_type=MESH,
        )

    def project(t, carry):
        cols = pl.ds(pl.multiple_of(t * tile, tile), tile)
        total = jnp.dot(att[...], w[:, cols], preferred_element_type=jnp.float32)
        for d in range(n_head):
            part[t, d] = total[d * share:(d + 1) * share].astype(jnp.bfloat16)

        @pl.when(t >= 1)
        def _():
            for step in range(1, n_head):
                give(t - 1, step).start()
        return carry
    lax.fori_loop(0, tiles, project, 0)
    for step in range(1, n_head):
        give(tiles - 1, step).start()

    def finish(t, carry):
        total = part[t, side].astype(jnp.float32)
        for step in range(1, n_head):
            give(t, step).wait_recv()
            total = total + got[t, step - 1].astype(jnp.float32)
        out_ref[:, pl.ds(pl.multiple_of(t * tile, tile), tile)] = total.astype(jnp.bfloat16)
        return carry
    lax.fori_loop(0, tiles, finish, 0)

    def sent(kind, plane, source, c, target):
        send(kind, held(plane, source, c), plane, source, c, target).wait_send()

    def drain(c):
        @pl.when(z + 1 < n_z)
        def _():
            sent(0, 1, p, c, me + PLANE)

        @pl.when(z >= x_old)
        def _():
            sent(2, x_old, p, c, base + px)

        @pl.when(z >= y_old)
        def _():
            sent(3, y_old, p, c, base + py)

        @pl.when(z >= 1)
        def _():
            @pl.when(z + 1 < n_z)
            def _():
                sent(1, 2, p, c, me + PLANE)
            sent(4, 1, p, c, base + px)
            sent(5, 1, p, c, base + py)
            sent(6, 1, px, c, base + py)

        @pl.when(z >= y_from)
        def _():
            sent(7, y_from, py, c, base + px)
    each(drain)

    @pl.when(me == 0)
    def _():
        sink_copy(0, sink, base + px).wait_send()

    @pl.when(me <= 1)
    def _():
        sink_copy(1, sink, base + py).wait_send()

    @pl.when(z + 1 < n_z)
    def _():
        sink_copy(2, sink, me + PLANE).wait_send()

    def gone(t, carry):
        for step in range(1, n_head):
            give(t, step).wait_send()
        return carry
    lax.fori_loop(0, tiles, gone, 0)


def shards(n_seq, n_head, queries, key_rows, value_rows, windows, sink_counts, sink_bias, out_weight):
    rows, heads, width = queries.shape
    kv_heads = key_rows.shape[1]
    group = heads // kv_heads
    lanes = group * rows
    depth, model = out_weight.shape
    assert (WINDOW - 1) // rows + 1 == 2 * PLANE and n_seq % PLANE == 0
    keys, values = key_rows.transpose(1, 0, 2), value_rows.transpose(1, 0, 2)
    q = queries.transpose(1, 0, 2).reshape(kv_heads, lanes, width)
    tile = min(512, model)
    tiles = model // tile
    share = rows // n_head
    bf16, f32, i32 = jnp.bfloat16, jnp.float32, jnp.int32
    vmem = pl.BlockSpec(memory_space=pltpu.VMEM)
    smem = pl.BlockSpec(memory_space=pltpu.SMEM)
    dma = pltpu.SemaphoreType.DMA
    return pl.pallas_call(
        functools.partial(kernel, n_seq, n_head, tile),
        out_shape=jax.ShapeDtypeStruct((share, model), bf16),
        in_specs=[smem, smem, smem] + [pl.BlockSpec(memory_space=pl.ANY)] * 4,
        out_specs=vmem,
        scratch_shapes=[
            pltpu.VMEM((kv_heads, 2, rows, width), bf16),
            pltpu.VMEM((kv_heads, lanes, width), bf16),
            pltpu.VMEM((3 * PLANE, kv_heads, 2, rows, width), bf16),
            pltpu.VMEM((kv_heads, 2, SINK_ROWS, width), bf16),
            pltpu.VMEM((kv_heads, width, lanes), bf16),
            pltpu.VMEM((kv_heads, 1, lanes), i32),
            pltpu.VMEM((kv_heads, 1, lanes), i32),
            pltpu.VMEM((kv_heads, 1, lanes), f32),
            pltpu.VMEM((kv_heads, 1, lanes), f32),
            pltpu.VMEM((kv_heads, 1, lanes), f32),
            pltpu.VMEM((kv_heads, width, lanes), f32),
            pltpu.VMEM((rows, depth), bf16),
            pltpu.VMEM((depth, model), bf16),
            pltpu.VMEM((tiles, n_head, share, tile), bf16),
            pltpu.VMEM((tiles, n_head - 1, share, tile), bf16),
            dma((8, kv_heads)),
            dma((3 * PLANE, kv_heads)),
            dma((3,)),
            dma,
            dma((kv_heads, 2)),
            dma,
            dma,
            dma((tiles, n_head - 1)),
            dma((tiles, n_head - 1)),
        ],
        compiler_params=pltpu.CompilerParams(
            collective_id=0, has_side_effects=True, vmem_limit_bytes=56 * 1024 * 1024
        ),
    )(windows, sink_counts, sink_bias, keys, values, q, out_weight)


def solution(mesh):
    in_specs = (
        P("seq", "head", None),
        P("seq", "head", None),
        P("seq", "head", None),
        P("head"),
        P("head"),
        P("head"),
        P("head", None),
    )
    body = functools.partial(shards, mesh.shape["seq"], mesh.shape["head"])
    out_specs = P(("seq", "head"), None)
    return jax.shard_map(body, mesh=mesh, in_specs=in_specs, out_specs=out_specs, check_vma=False)
```

profile of v0, /device:TPU:27, one launch (start us, length us, event | category | flops | bytes accessed | tf_op | source)
XLA Modules:
  0.0 60.8 jit_solution(8233512695109763547)
XLA Ops:
  0.0 1.8 %copy_bitcast_fusion = (bf16[4,192,128]{2,1,0:T(8,128)(2,1)}, bf16[4,192,128]{2,1,0:T(8,128)(2,1)}) fusion(bf16[192,4,128]{2,1,0:T(4,128)(2,1)} %param.9, bf16[192,4,128]{2,1,0:T(4,128)(2,1)} %param.8), kind=kLoop, calls=%fused_computation | loop fusion | bytes 786432 | tf_op jit(solution)/shard_map/transpose | solution.py:387
  1.8 2.2 %copy.10 = bf16[16,192,128]{2,1,0:T(8,128)(2,1)} copy(bf16[16,192,128]{2,0,1:T(8,128)(2,1)} %bitcast.7) | data formatting | bytes 1572864 | tf_op jit(solution)/shard_map/transpose | solution.py:388
  4.0 54.7 %shard_map.73 = bf16[96,4096]{1,0:T(8,128)(2,1)} custom-call(s32[16]{0:T(128)} %win_ref.1, s32[16]{0:T(128)} %cnt_ref.1, f32[16]{0:T(128)} %bias_ref.1, bf16[4,192,128]{2,1,0:T(8,128)(2,1)} %get-tuple-element.6.k_hbm, bf16[4,192,128]{2,1,0:T(8,128)(2,1)} %get-tuple-element.5.v_hbm, bf16[4,768,128]{2,1,0:T(8,128)(2,1)} %bitcast.6, bf16[2048,4096]{1,0:T(8,128)(2,1)} %w_hbm.1), custom_call_target="tpu_custom_call" | custom-call | tf_op jit(solution)/shard_map/pallas_call | solution.py:396
  58.7 2.1 %copy.14 = bf16[96,4096]{1,0:T(8,128)(2,1)} copy(bf16[96,4096]{1,0:T(8,128)(2,1)} %shard_map.73) | data formatting | bytes 1572864
where the time goes:
time: 61.1 us; the launch traced here: 60.8 us
  Pallas kernels  54.7 us (90%)
  local copies, waits for them, and re-layouts  6.09 us (10%)
    pallas_call x1, Pallas kernels, shards(): pl.pallas_call(functools.partial(kernel, n_seq, n_head, tile), out_shape=...  54.7 us
    transpose x1, local copies, waits for them, and re-layouts, shards(): q = queries.transpose(1, 0, 2).reshape(kv_heads, lanes, width)  2.22 us
    unnamed x1, local copies, waits for them, and re-layouts  2.06 us
    transpose x1, local copies, waits for them, and re-layouts, shards(): keys, values = (key_rows.transpose(1, 0, 2), value_rows.transpose(1, 0, 2))  1.81 us

commit v1 on v0

--- a/solution.py
+++ b/solution.py
@@ -1,4 +1,5 @@
 import functools
+import heapq
 
 import jax
 import jax.numpy as jnp
@@ -15,18 +16,94 @@
 LOG2E = 1.4426950408889634
 MESH = pl.DeviceIdType.MESH
 
+KINDS = 8
+SINK_EARLY, SINK_MID, SINK_LATE, CLOSE = 8, 9, 10, 11
+CHUNK_US, HOP_US = 2.1, 1.7
+BITS, PER_WORD = 6, 5
+
+
+def kinds_of(p):
+    b0, b1 = p % 2, p // 2
+    px, py, pd = p ^ 1, p ^ 2, 3 - p
+    return [(1, p), (2, p), (1, px), (1, py), (1, pd), (2 - 2 * b0, px), (2 - 2 * b1, py), (2 - 2 * b1, pd)]
+
+
+def forwards(z, p, plane, src):
+    b0, b1 = p % 2, p // 2
+    px, py = p ^ 1, p ^ 2
+    out = []
+    if (plane, src) == (0, p):
+        out.append(("z", z + 1, p, 1))
+        if b0 == 0:
+            out.append(("x", z, px, 0))
+        if b1 == 0:
+            out.append(("y", z, py, 0))
+    if (plane, src) == (1, p):
+        out += [("z", z + 1, p, 2), ("x", z, px, 1), ("y", z, py, 1)]
+    if (plane, src) == (2, p):
+        if b0 == 1:
+            out.append(("x", z, px, 2))
+        if b1 == 1:
+            out.append(("y", z, py, 2))
+    if (plane, src) == (1, px):
+        out.append(("y", z, py, 1))
+    if (plane, src) == (2 - 2 * b1, py):
+        out.append(("x", z, px, plane))
+    return out
+
+
+def arrivals(heads):
+    queue, free, landed, tick = [], {}, {}, 0
+    for c in range(heads):
+        for z in range(3):
+            for p in range(PLANE):
+                heapq.heappush(queue, (1e-3 * c, tick, z, p, 0, p, c))
+                tick += 1
+    while queue:
+        t, _, z, p, plane, src, c = heapq.heappop(queue)
+        landed[z, p, plane, src, c] = t
+        for link, z_to, p_to, plane_to in forwards(z, p, plane, src):
+            if z_to < 3:
+                start = max(t, free.get((z, p, link), 0.0))
+                free[z, p, link] = start + CHUNK_US
+                heapq.heappush(queue, (start + CHUNK_US + HOP_US, tick, z_to, p_to, plane_to, src, c))
+                tick += 1
+    return landed
+
+
+def agenda(heads):
+    landed = arrivals(heads)
+    plans = []
+    for p in range(PLANE):
+        due = [(landed[2, p, plane, src, c], k, c) for k, (plane, src) in enumerate(kinds_of(p)) for c in range(heads)]
+        due += [(11.0, SINK_EARLY, 0), (19.3, SINK_MID, 0), (21.7, SINK_LATE, 0)]
+        due.sort()
+        last = [max(i for i, e in enumerate(due) if e[2] == c or e[1] == SINK_LATE) for c in range(heads)]
+        plan, ready = [], 0
+        for i, (_, k, c) in enumerate(due):
+            plan.append(k * heads + c)
+            while ready < heads - 1 and all(last[r] <= i for r in range(ready + 1)):
+                plan.append(CLOSE * heads + ready)
+                ready += 1
+        assert ready == heads - 1 and max(plan) < 1 << BITS
+        plans.append(plan)
+    return plans
+
 
 def kernel(
-    n_seq, n_head, tile,
+    n_seq, n_head, tile, wide, plans,
     win_ref, cnt_ref, bias_ref, k_hbm, v_hbm, q_hbm, w_hbm, out_ref,
-    own, q_ref, kv, sink, qt, low, few, lift, top, norm, acc, att, w, part, got,
-    send_sem, recv_sem, sink_send, sink_recv, own_sem, q_sem, w_sem, part_send, part_recv,
+    k_raw, v_raw, q_raw, k_wide, v_wide, q_wide,
+    own, kv, sink, qt, low, few, lift, top, norm, acc, att, w, total, part, got,
+    send_sem, recv_sem, sink_send, sink_recv, raw_sem, w_sem, part_send, part_recv,
 ):
     me, side = lax.axis_index("seq"), lax.axis_index("head")
     heads_kv, _, rows, width = own.shape
-    lanes = q_ref.shape[1]
+    lanes = qt.shape[2]
     group = lanes // rows
+    heads = heads_kv * group
     model = w.shape[1]
+    depth = group * width
     share = rows // n_head
     z, p = me // PLANE, lax.rem(me, PLANE)
     bit0, bit1 = lax.rem(p, 2), p // 2
@@ -43,13 +120,11 @@
 
     above, below = (z + 1 < n_z).astype(jnp.int32), (z > 0).astype(jnp.int32)
     loads = [
-        pltpu.make_async_copy(ref.at[c], own.at[c, k], own_sem.at[c, k])
-        for c in range(heads_kv) for k, ref in enumerate((k_hbm, v_hbm))
+        pltpu.make_async_copy(source, target, raw_sem.at[i])
+        for i, (source, target) in enumerate(((k_hbm, k_raw), (v_hbm, v_raw), (q_hbm, q_raw)))
     ]
     for load in loads:
         load.start()
-    q_load = pltpu.make_async_copy(q_hbm, q_ref, q_sem)
-    q_load.start()
     greet({"seq": base + px})
     greet({"seq": base + py})
 
@@ -63,7 +138,6 @@
 
     for step in range(1, n_head):
         greet({"head": lax.rem(side + step, n_head)})
-    pl.semaphore_wait(barrier, n_head + 1 + above + below)
 
     def send(kind, src, plane, source, c, target):
         return pltpu.make_async_remote_copy(
@@ -81,8 +155,8 @@
     def held(plane, source, c):
         return kv.at[plane * PLANE + source, c]
 
-    x_old, y_old, d_old = 2 * bit0, 2 * bit1, 2 * bit1
-    x_from, y_from, d_from = 2 - 2 * bit0, 2 - 2 * bit1, 2 - 2 * bit1
+    x_old, y_old = 2 * bit0, 2 * bit1
+    x_from, y_from = 2 - 2 * bit0, 2 - 2 * bit1
 
     def sink_copy(way, source, target):
         return pltpu.make_async_remote_copy(
@@ -96,8 +170,23 @@
 
     first_rows = own.at[:, :, pl.ds(0, SINK_ROWS)]
 
-    for load in loads:
-        load.wait()
+    for i, (raw, spread) in enumerate(((k_raw, k_wide), (v_raw, v_wide))):
+        loads[i].wait()
+        spread[...] = raw[...].astype(jnp.float32)
+        for c in range(heads_kv):
+            own[c, i] = spread[pl.ds(c, rows, stride=heads_kv), :].astype(jnp.bfloat16)
+    pl.semaphore_wait(barrier, n_head + 1 + above + below)
+
+    @pl.when(me == 0)
+    def _():
+        sink_copy(0, first_rows, base + px).start()
+        sink_copy(1, first_rows, base + py).start()
+
+        @pl.when(z + 1 < n_z)
+        def _():
+            sink_copy(2, first_rows, me + PLANE).start()
+        sink[...] = own[:, :, :SINK_ROWS]
+
     for c in range(heads_kv):
         @pl.when(z + 1 < n_z)
         def _():
@@ -111,20 +200,14 @@
         def _():
             send(3, own.at[c], 0, p, c, base + py).start()
 
-        if c == 0:
-            @pl.when(me == 0)
-            def _():
-                sink_copy(0, first_rows, base + px).start()
-                sink_copy(1, first_rows, base + py).start()
-
-                @pl.when(z + 1 < n_z)
-                def _():
-                    sink_copy(2, first_rows, me + PLANE).start()
-
-    fetch = pltpu.make_async_copy(w_hbm, w, w_sem)
-    fetch.start()
-
-    q_load.wait()
+    def fetch(c):
+        part_of = pl.ds(pl.multiple_of(c * depth, depth), depth)
+        return pltpu.make_async_copy(w_hbm.at[part_of], w.at[part_of], w_sem.at[c])
+
+    loads[2].wait()
+    for c in range(heads_kv):
+        fetch(c).start()
+    q_wide[...] = q_raw[...].astype(jnp.float32)
     column = lax.broadcasted_iota(jnp.int32, (1, lanes), 1)
     for c in range(heads_kv):
         window, count, bias, token = (jnp.zeros((1, lanes), t) for t in (jnp.int32, jnp.int32, jnp.float32, jnp.int32))
@@ -139,7 +222,8 @@
         low[c] = jnp.maximum(token - window, count - 1)
         few[c] = jnp.minimum(token, count - 1)
         lift[c] = bias * LOG2E
-        qt[c] = q_ref[c].T
+        picked = [q_wide[pl.ds(c * group + g, rows, stride=heads), :].astype(jnp.bfloat16) for g in range(group)]
+        qt[c] = jnp.concatenate(picked, axis=0).T
         top[c] = jnp.full((1, lanes), HIDDEN, jnp.float32)
         norm[c] = jnp.zeros((1, lanes), jnp.float32)
         acc[c] = jnp.zeros((width, lanes), jnp.float32)
@@ -170,9 +254,9 @@
             fades.append(jnp.exp2(old - new))
             sums.append(jnp.sum(e, axis=0, keepdims=True))
         adds = [jnp.dot(turned, e, preferred_element_type=jnp.float32) for e in weights]
-        for new, fade, total, add, cols in zip(news, fades, sums, adds, parts):
+        for new, fade, added, add, cols in zip(news, fades, sums, adds, parts):
             top[c, :, cols] = new
-            norm[c, :, cols] = norm[c, :, cols] * fade + total
+            norm[c, :, cols] = norm[c, :, cols] * fade + added
             acc[c, :, cols] = acc[c, :, cols] * fade + add
 
     def each(body):
@@ -182,20 +266,7 @@
         lax.fori_loop(0, heads_kv, one, 0)
 
     each(lambda c: attend(own.at[c], c, me, causal=True))
-
-    @pl.when(z >= 1)
-    def _():
-        def first(c):
-            landed(1, p, c)
-
-            @pl.when(z + 1 < n_z)
-            def _():
-                send(1, held(1, p, c), 2, p, c, me + PLANE).start()
-
-            send(4, held(1, p, c), 1, p, c, base + px).start()
-            send(5, held(1, p, c), 1, p, c, base + py).start()
-            attend(held(1, p, c), c, me - PLANE)
-        each(first)
+    total[...] = jnp.zeros(total.shape, jnp.float32)
 
     def pass_on():
         sink_copy(0, sink, me).wait_recv()
@@ -208,89 +279,94 @@
         def _():
             sink_copy(2, sink, me + PLANE).start()
 
-    @pl.when((me > 0) & (z <= 1))
-    def _():
-        pass_on()
-
-    @pl.when(z >= 1)
-    def _():
-        def second(c):
-            @pl.when(z >= 2)
-            def _():
-                landed(2, p, c)
-
-                @pl.when(x_old == 2)
-                def _():
-                    send(2, held(2, p, c), 2, p, c, base + px).start()
-
-                @pl.when(y_old == 2)
-                def _():
-                    send(3, held(2, p, c), 2, p, c, base + py).start()
-
-            landed(1, px, c)
-            send(6, held(1, px, c), 1, px, c, base + py).start()
-            attend(held(1, px, c), c, base - PLANE + px)
-        each(second)
-
-    def relay(c):
-        @pl.when(z >= y_from)
-        def _():
-            landed(y_from, py, c)
-            send(7, held(y_from, py, c), y_from, py, c, base + px).start()
-            attend(held(y_from, py, c), c, base - y_from * PLANE + py)
-    each(relay)
-
-    @pl.when(z >= 2)
-    def _():
-        pass_on()
-
-    @pl.when(me == 0)
-    def _():
-        each(lambda c: attend(own.at[c, :, pl.ds(0, SINK_ROWS)], c, 0, sinks=True))
-
-    @pl.when(me > 0)
-    def _():
-        each(lambda c: attend(sink.at[c], c, 0, sinks=True))
-
-    @pl.when(z >= 2)
-    def _():
-        each(lambda c: attend(held(2, p, c), c, me - 2 * PLANE))
-
-    @pl.when(z >= 1)
-    def _():
-        def third(c):
-            landed(1, py, c)
-            attend(held(1, py, c), c, base - PLANE + py)
-        each(third)
-
-    @pl.when(z >= x_from)
-    def _():
-        def fourth(c):
-            landed(x_from, px, c)
-            attend(held(x_from, px, c), c, base - x_from * PLANE + px)
-        each(fourth)
-
-    @pl.when(z >= 1)
-    def _():
-        def fifth(c):
-            landed(1, pd, c)
-            attend(held(1, pd, c), c, base - PLANE + pd)
-        each(fifth)
-
-    @pl.when(z >= d_from)
-    def _():
-        def sixth(c):
-            landed(d_from, pd, c)
-            attend(held(d_from, pd, c), c, base - d_from * PLANE + pd)
-        each(sixth)
-
-    for c in range(heads_kv):
+    def close(c):
         mixed = (acc[c] / norm[c]).T.astype(jnp.bfloat16)
         for g in range(group):
-            h = c * group + g
-            att[:, h * width:(h + 1) * width] = mixed[g * rows:(g + 1) * rows]
-
-    fetch.wait()
+            att[:, g * width:(g + 1) * width] = mixed[g * rows:(g + 1) * rows]
+        fetch(c).wait()
+
+    def rows_of(c):
+        return pl.ds(pl.multiple_of(c * depth, depth), depth)
+
+    n_words = (max(len(plan) for plan in plans) + PER_WORD - 1) // PER_WORD
+    words = []
+    for i in range(n_words):
+        packed = []
+        for plan in plans:
+            value = 0
+            for j, code in enumerate(plan[i * PER_WORD:(i + 1) * PER_WORD]):
+                value += code << (BITS * j)
+            packed.append(value)
+        word = jnp.int32(packed[0])
+        for q in range(1, PLANE):
+            word = jnp.where(p == q, jnp.int32(packed[q]), word)
+        words.append(word)
+
+    def pick(index, choices):
+        chosen = choices[-1]
+        for i in range(len(choices) - 2, -1, -1):
+            chosen = jnp.where(index == i, choices[i], chosen)
+        return chosen
+
+    def event(i, carry):
+        word = pick(i // PER_WORD, words)
+        code = lax.shift_right_logical(word, BITS * lax.rem(i, PER_WORD)) & ((1 << BITS) - 1)
+        kind, c = code // heads_kv, lax.rem(code, heads_kv)
+        plane = pick(kind, [1, 2, 1, 1, 1, x_from, y_from, y_from])
+        source = pick(kind, [p, p, px, py, pd, px, py, pd])
+
+        @pl.when((kind < KINDS) & (z >= plane))
+        def _():
+            landed(plane, source, c)
+
+            @pl.when(kind == 0)
+            def _():
+                @pl.when(z + 1 < n_z)
+                def _():
+                    send(1, held(1, p, c), 2, p, c, me + PLANE).start()
+                send(4, held(1, p, c), 1, p, c, base + px).start()
+                send(5, held(1, p, c), 1, p, c, base + py).start()
+
+            @pl.when((kind == 1) & (x_old == 2))
+            def _():
+                send(2, held(2, p, c), 2, p, c, base + px).start()
+
+            @pl.when((kind == 1) & (y_old == 2))
+            def _():
+                send(3, held(2, p, c), 2, p, c, base + py).start()
+
+            @pl.when(kind == 2)
+            def _():
+                send(6, held(1, px, c), 1, px, c, base + py).start()
+
+            @pl.when(kind == 6)
+            def _():
+                send(7, held(y_from, py, c), y_from, py, c, base + px).start()
+
+            attend(held(plane, source, c), c, base - plane * PLANE + source)
+
+        turn = jnp.where(z <= 1, SINK_EARLY, jnp.where(z == 2, SINK_MID, SINK_LATE))
+
+        @pl.when(kind == turn)
+        def _():
+            @pl.when(me > 0)
+            def _():
+                pass_on()
+            each(lambda c: attend(sink.at[c], c, 0, sinks=True))
+
+        @pl.when(kind == CLOSE)
+        def _():
+            close(c)
+
+            def project(t, carry):
+                cols = pl.ds(pl.multiple_of(t * wide, wide), wide)
+                total[:, cols] += jnp.dot(att[...], w[rows_of(c), cols], preferred_element_type=jnp.float32)
+                return carry
+            lax.fori_loop(0, model // wide, project, 0)
+        return carry
+    lax.fori_loop(0, len(plans[0]), event, 0)
+
+    close(heads_kv - 1)
     tiles = model // tile
 
     def give(t, step):
@@ -306,9 +382,9 @@
 
     def project(t, carry):
         cols = pl.ds(pl.multiple_of(t * tile, tile), tile)
-        total = jnp.dot(att[...], w[:, cols], preferred_element_type=jnp.float32)
+        whole = total[:, cols] + jnp.dot(att[...], w[rows_of(heads_kv - 1), cols], preferred_element_type=jnp.float32)
         for d in range(n_head):
-            part[t, d] = total[d * share:(d + 1) * share].astype(jnp.bfloat16)
+            part[t, d] = whole[d * share:(d + 1) * share].astype(jnp.bfloat16)
 
         @pl.when(t >= 1)
         def _():
@@ -320,11 +396,11 @@
         give(tiles - 1, step).start()
 
     def finish(t, carry):
-        total = part[t, side].astype(jnp.float32)
+        whole = part[t, side].astype(jnp.float32)
         for step in range(1, n_head):
             give(t, step).wait_recv()
-            total = total + got[t, step - 1].astype(jnp.float32)
-        out_ref[:, pl.ds(pl.multiple_of(t * tile, tile), tile)] = total.astype(jnp.bfloat16)
+            whole = whole + got[t, step - 1].astype(jnp.float32)
+        out_ref[:, pl.ds(pl.multiple_of(t * tile, tile), tile)] = whole.astype(jnp.bfloat16)
         return carry
     lax.fori_loop(0, tiles, finish, 0)
 
@@ -384,9 +460,7 @@
     lanes = group * rows
     depth, model = out_weight.shape
     assert (WINDOW - 1) // rows + 1 == 2 * PLANE and n_seq % PLANE == 0
-    keys, values = key_rows.transpose(1, 0, 2), value_rows.transpose(1, 0, 2)
-    q = queries.transpose(1, 0, 2).reshape(kv_heads, lanes, width)
-    tile = min(512, model)
+    tile, wide = min(512, model), min(1024, model)
     tiles = model // tile
     share = rows // n_head
     bf16, f32, i32 = jnp.bfloat16, jnp.float32, jnp.int32
@@ -394,13 +468,18 @@
     smem = pl.BlockSpec(memory_space=pltpu.SMEM)
     dma = pltpu.SemaphoreType.DMA
     return pl.pallas_call(
-        functools.partial(kernel, n_seq, n_head, tile),
+        functools.partial(kernel, n_seq, n_head, tile, wide, agenda(kv_heads)),
         out_shape=jax.ShapeDtypeStruct((share, model), bf16),
         in_specs=[smem, smem, smem] + [pl.BlockSpec(memory_space=pl.ANY)] * 4,
         out_specs=vmem,
         scratch_shapes=[
+            pltpu.VMEM((rows * kv_heads, width), bf16),
+            pltpu.VMEM((rows * kv_heads, width), bf16),
+            pltpu.VMEM((rows * heads, width), bf16),
+            pltpu.VMEM((rows * kv_heads, width), f32),
+            pltpu.VMEM((rows * kv_heads, width), f32),
+            pltpu.VMEM((rows * heads, width), f32),
             pltpu.VMEM((kv_heads, 2, rows, width), bf16),
-            pltpu.VMEM((kv_heads, lanes, width), bf16),
             pltpu.VMEM((3 * PLANE, kv_heads, 2, rows, width), bf16),
             pltpu.VMEM((kv_heads, 2, SINK_ROWS, width), bf16),
             pltpu.VMEM((kv_heads, width, lanes), bf16),
@@ -410,24 +489,32 @@
             pltpu.VMEM((kv_heads, 1, lanes), f32),
             pltpu.VMEM((kv_heads, 1, lanes), f32),
             pltpu.VMEM((kv_heads, width, lanes), f32),
-            pltpu.VMEM((rows, depth), bf16),
+            pltpu.VMEM((rows, group * width), bf16),
             pltpu.VMEM((depth, model), bf16),
+            pltpu.VMEM((rows, model), f32),
             pltpu.VMEM((tiles, n_head, share, tile), bf16),
             pltpu.VMEM((tiles, n_head - 1, share, tile), bf16),
             dma((8, kv_heads)),
             dma((3 * PLANE, kv_heads)),
             dma((3,)),
             dma,
-            dma((kv_heads, 2)),
-            dma,
-            dma,
+            dma((3,)),
+            dma((kv_heads,)),
             dma((tiles, n_head - 1)),
             dma((tiles, n_head - 1)),
         ],
         compiler_params=pltpu.CompilerParams(
             collective_id=0, has_side_effects=True, vmem_limit_bytes=56 * 1024 * 1024
         ),
-    )(windows, sink_counts, sink_bias, keys, values, q, out_weight)
+    )(
+        windows,
+        sink_counts,
+        sink_bias,
+        key_rows.reshape(rows * kv_heads, width),
+        value_rows.reshape(rows * kv_heads, width),
+        queries.reshape(rows * heads, width),
+        out_weight,
+    )
 
 
 def solution(mesh):

time: 61.1 us -> 49.3 us (0.81)
  the two profiles are of different devices: /device:TPU:27 before, /device:TPU:17 now
where the time goes in v1:
time: 49.3 us; the launch traced here: 48.6 us
  Pallas kernels  46.6 us (95%)
  local copies, waits for them, and re-layouts  2.06 us (4%)
    pallas_call x1, Pallas kernels, shards(): pl.pallas_call(functools.partial(kernel, n_seq, n_head, tile, wide, agend...  46.6 us
    unnamed x1, local copies, waits for them, and re-layouts  2.06 us

profile of v1, /device:TPU:17, one launch (start us, length us, event | category | flops | bytes accessed | tf_op | source)
XLA Modules:
  0.0 48.6 jit_solution(6805289964060392781)
XLA Ops:
  0.0 46.6 %shard_map.73 = bf16[96,4096]{1,0:T(8,128)(2,1)} custom-call(s32[16]{0:T(128)} %win_ref.1, s32[16]{0:T(128)} %cnt_ref.1, f32[16]{0:T(128)} %bias_ref.1, bf16[768,128]{1,0:T(8,128)(2,1)} %bitcast.4, bf16[768,128]{1,0:T(8,128)(2,1)} %bitcast.5, bf16[3072,128]{1,0:T(8,128)(2,1)} %bitcast.3, bf16[2048,4096]{1,0:T(8,128)(2,1)} %w_hbm.1), custom_call_target="tpu_custom_call" | custom-call | tf_op jit(solution)/shard_map/pallas_call | solution.py:470
  46.6 2.1 %copy.9 = bf16[96,4096]{1,0:T(8,128)(2,1)} copy(bf16[96,4096]{1,0:T(8,128)(2,1)} %shard_map.73) | data formatting | bytes 1572864

commit v2 on v1

--- a/solution.py
+++ b/solution.py
@@ -17,7 +17,9 @@
 MESH = pl.DeviceIdType.MESH
 
 KINDS = 8
-SINK_EARLY, SINK_MID, SINK_LATE, CLOSE = 8, 9, 10, 11
+PAIRS = KINDS // 2
+PAIR = KINDS
+SINK_EARLY, SINK_MID, SINK_LATE = PAIR + PAIRS, PAIR + PAIRS + 1, PAIR + PAIRS + 2
 CHUNK_US, HOP_US = 2.1, 1.7
 BITS, PER_WORD = 6, 5
 
@@ -73,25 +75,27 @@
 
 def agenda(heads):
     landed = arrivals(heads)
-    plans = []
+    plans, orders = [], []
     for p in range(PLANE):
-        due = [(landed[2, p, plane, src, c], k, c) for k, (plane, src) in enumerate(kinds_of(p)) for c in range(heads)]
+        kinds = kinds_of(p)
+        when = [[landed[2, p, plane, src, c] for c in range(heads)] for plane, src in kinds]
+        order = sorted(range(KINDS), key=lambda k: (sum(when[k]), k))
+        due = [(when[k][c], k, c) for k in range(KINDS) for c in range(heads)]
         due += [(11.0, SINK_EARLY, 0), (19.3, SINK_MID, 0), (21.7, SINK_LATE, 0)]
-        due.sort()
-        last = [max(i for i, e in enumerate(due) if e[2] == c or e[1] == SINK_LATE) for c in range(heads)]
-        plan, ready = [], 0
-        for i, (_, k, c) in enumerate(due):
-            plan.append(k * heads + c)
-            while ready < heads - 1 and all(last[r] <= i for r in range(ready + 1)):
-                plan.append(CLOSE * heads + ready)
-                ready += 1
-        assert ready == heads - 1 and max(plan) < 1 << BITS
-        plans.append(plan)
-    return plans
+        for j in range(PAIRS):
+            for c in range(heads):
+                if j < PAIRS - 1 or c < heads - 1:
+                    ready = max(when[k][c] for k in order[2 * j:2 * j + 2])
+                    due.append((max(ready, 21.7) if j == PAIRS - 1 else ready, PAIR + j, c))
+        due.sort(key=lambda e: (e[0], PAIR <= e[1] < SINK_EARLY, e[1], e[2]))
+        plans.append([k * heads + c for _, k, c in due])
+        assert max(plans[-1]) < 1 << BITS
+        orders.append(order)
+    return plans, orders
 
 
 def kernel(
-    n_seq, n_head, tile, wide, plans,
+    n_seq, n_head, tile, wide, plans, orders,
     win_ref, cnt_ref, bias_ref, k_hbm, v_hbm, q_hbm, w_hbm, out_ref,
     k_raw, v_raw, q_raw, k_wide, v_wide, q_wide,
     own, kv, sink, qt, low, few, lift, top, norm, acc, att, w, total, part, got,
@@ -228,36 +232,51 @@
         norm[c] = jnp.zeros((1, lanes), jnp.float32)
         acc[c] = jnp.zeros((width, lanes), jnp.float32)
 
-    def attend(block, c, shard, causal=False, sinks=False):
-        keys, values = block[0], block[1]
-        key_row = lax.broadcasted_iota(jnp.int32, (keys.shape[0], 1), 0)
-        step = min(256, lanes)
-        parts = [slice(n, n + step) for n in range(0, lanes, step)]
-        scores = [jnp.dot(keys, qt[c, :, cols], preferred_element_type=jnp.float32) for cols in parts]
-        turned = values.T
+    step = min(256, lanes)
+    parts = [slice(n, n + step) for n in range(0, lanes, step)]
+
+    def attend(blocks, c, shards, causal=False, last=False):
+        keys = [block[0] for block in blocks] + ([sink[c, 0]] if last else [])
+        values = [block[1] for block in blocks] + ([sink[c, 1]] if last else [])
+        turned = jnp.concatenate(values, axis=0).T
+        key_row = lax.broadcasted_iota(jnp.int32, (rows, 1), 0)
+        scores = [[jnp.dot(k, qt[c, :, cols], preferred_element_type=jnp.float32) for k in keys] for cols in parts]
         olds = [top[c, :, cols] for cols in parts]
         weights, news, fades, sums = [], [], [], []
-        for s, old, cols in zip(scores, olds, parts):
-            s = s * scale
-            if sinks:
-                s = jnp.where(key_row <= few[c, :, cols], s + lift[c, :, cols], HIDDEN)
-            else:
+        for pieces, old, cols in zip(scores, olds, parts):
+            shown = []
+            for s, shard in zip(pieces, shards):
                 seen = key_row > low[c, :, cols] - shard * rows
                 if causal:
                     column = lax.broadcasted_iota(jnp.int32, (1, step), 1) + cols.start
                     seen = seen & (key_row <= lax.rem(column, rows))
-                s = jnp.where(seen, s, HIDDEN)
-            new = jnp.maximum(old, jnp.max(s, axis=0, keepdims=True))
-            e = jnp.exp2(s - new)
-            weights.append(e.astype(jnp.bfloat16))
+                shown.append(jnp.where(seen, s * scale, HIDDEN))
+            if last:
+                sink_row = lax.broadcasted_iota(jnp.int32, (SINK_ROWS, 1), 0)
+                shown.append(jnp.where(sink_row <= few[c, :, cols], pieces[-1] * scale + lift[c, :, cols], HIDDEN))
+            new = old
+            for s in shown:
+                new = jnp.maximum(new, jnp.max(s, axis=0, keepdims=True))
+            e = [jnp.exp2(s - new) for s in shown]
+            weights.append(jnp.concatenate([x.astype(jnp.bfloat16) for x in e], axis=0))
             news.append(new)
             fades.append(jnp.exp2(old - new))
-            sums.append(jnp.sum(e, axis=0, keepdims=True))
+            sums.append(functools.reduce(jnp.add, [jnp.sum(x, axis=0, keepdims=True) for x in e]))
         adds = [jnp.dot(turned, e, preferred_element_type=jnp.float32) for e in weights]
+        mixed = []
         for new, fade, added, add, cols in zip(news, fades, sums, adds, parts):
-            top[c, :, cols] = new
-            norm[c, :, cols] = norm[c, :, cols] * fade + added
-            acc[c, :, cols] = acc[c, :, cols] * fade + add
+            whole = acc[c, :, cols] * fade + add
+            weight = norm[c, :, cols] * fade + added
+            if last:
+                mixed.append((whole * (1.0 / weight)).T.astype(jnp.bfloat16))
+            else:
+                top[c, :, cols] = new
+                norm[c, :, cols] = weight
+                acc[c, :, cols] = whole
+        if last:
+            mixed = jnp.concatenate(mixed, axis=0)
+            for g in range(group):
+                att[:, g * width:(g + 1) * width] = mixed[g * rows:(g + 1) * rows]
 
     def each(body):
         def one(c, carry):
@@ -265,8 +284,15 @@
             return carry
         lax.fori_loop(0, heads_kv, one, 0)
 
-    each(lambda c: attend(own.at[c], c, me, causal=True))
+    each(lambda c: attend([own.at[c]], c, [me], causal=True))
     total[...] = jnp.zeros(total.shape, jnp.float32)
+
+    @pl.when(z < 2)
+    def _():
+        def clear(i, carry):
+            kv[i // heads_kv, lax.rem(i, heads_kv)] = jnp.zeros(own.shape[1:], jnp.bfloat16)
+            return carry
+        lax.fori_loop((z + 1) * PLANE * heads_kv, 3 * PLANE * heads_kv, clear, 0)
 
     def pass_on():
         sink_copy(0, sink, me).wait_recv()
@@ -279,28 +305,23 @@
         def _():
             sink_copy(2, sink, me + PLANE).start()
 
-    def close(c):
-        mixed = (acc[c] / norm[c]).T.astype(jnp.bfloat16)
-        for g in range(group):
-            att[:, g * width:(g + 1) * width] = mixed[g * rows:(g + 1) * rows]
-        fetch(c).wait()
-
     def rows_of(c):
         return pl.ds(pl.multiple_of(c * depth, depth), depth)
 
-    n_words = (max(len(plan) for plan in plans) + PER_WORD - 1) // PER_WORD
-    words = []
-    for i in range(n_words):
-        packed = []
-        for plan in plans:
-            value = 0
-            for j, code in enumerate(plan[i * PER_WORD:(i + 1) * PER_WORD]):
-                value += code << (BITS * j)
-            packed.append(value)
-        word = jnp.int32(packed[0])
+    def at_position(choices):
+        chosen = jnp.int32(choices[0])
         for q in range(1, PLANE):
-            word = jnp.where(p == q, jnp.int32(packed[q]), word)
-        words.append(word)
+            chosen = jnp.where(p == q, jnp.int32(choices[q]), chosen)
+        return chosen
+
+    def packed(codes, bits):
+        return sum(code << (bits * j) for j, code in enumerate(codes))
+
+    n_words = (len(plans[0]) + PER_WORD - 1) // PER_WORD
+    words = [
+        at_position([packed(plan[i * PER_WORD:(i + 1) * PER_WORD], BITS) for plan in plans]) for i in range(n_words)
+    ]
+    landing = at_position([packed(order, 3) for order in orders])
 
     def pick(index, choices):
         chosen = choices[-1]
@@ -308,12 +329,29 @@
             chosen = jnp.where(index == i, choices[i], chosen)
         return chosen
 
+    def where_is(kind):
+        return pick(kind, [1, 2, 1, 1, 1, x_from, y_from, y_from]), pick(kind, [p, p, px, py, pd, px, py, pd])
+
+    def pair(j, c, last=False):
+        blocks, shards, nearest = [], [], 2
+        for i in range(2):
+            plane, source = where_is(lax.shift_right_logical(landing, 3 * (2 * j + i)) & 7)
+            blocks.append(held(plane, source, c))
+            shards.append(base - plane * PLANE + source)
+            nearest = jnp.minimum(nearest, plane)
+        if last:
+            attend(blocks, c, shards, last=True)
+            fetch(c).wait()
+        else:
+            @pl.when(z >= nearest)
+            def _():
+                attend(blocks, c, shards)
+
     def event(i, carry):
         word = pick(i // PER_WORD, words)
         code = lax.shift_right_logical(word, BITS * lax.rem(i, PER_WORD)) & ((1 << BITS) - 1)
         kind, c = code // heads_kv, lax.rem(code, heads_kv)
-        plane = pick(kind, [1, 2, 1, 1, 1, x_from, y_from, y_from])
-        source = pick(kind, [p, p, px, py, pd, px, py, pd])
+        plane, source = where_is(kind)
 
         @pl.when((kind < KINDS) & (z >= plane))
         def _():
@@ -343,20 +381,19 @@
             def _():
                 send(7, held(y_from, py, c), y_from, py, c, base + px).start()
 
-            attend(held(plane, source, c), c, base - plane * PLANE + source)
-
         turn = jnp.where(z <= 1, SINK_EARLY, jnp.where(z == 2, SINK_MID, SINK_LATE))
 
-        @pl.when(kind == turn)
-        def _():
-            @pl.when(me > 0)
-            def _():
-                pass_on()
-            each(lambda c: attend(sink.at[c], c, 0, sinks=True))
-
-        @pl.when(kind == CLOSE)
-        def _():
-            close(c)
+        @pl.when((kind == turn) & (me > 0))
+        def _():
+            pass_on()
+
+        @pl.when((kind >= PAIR) & (kind < PAIR + PAIRS - 1))
+        def _():
+            pair(kind - PAIR, c)
+
+        @pl.when(kind == PAIR + PAIRS - 1)
+        def _():
+            pair(PAIRS - 1, c, last=True)
 
             def project(t, carry):
                 cols = pl.ds(pl.multiple_of(t * wide, wide), wide)
@@ -366,7 +403,7 @@
         return carry
     lax.fori_loop(0, len(plans[0]), event, 0)
 
-    close(heads_kv - 1)
+    pair(PAIRS - 1, heads_kv - 1, last=True)
     tiles = model // tile
 
     def give(t, step):
@@ -395,6 +432,48 @@
     for step in range(1, n_head):
         give(tiles - 1, step).start()
 
+    def sent(kind, plane, source, c, target):
+        send(kind, held(plane, source, c), plane, source, c, target).wait_send()
+
+    def drain(c):
+        @pl.when(z + 1 < n_z)
+        def _():
+            sent(0, 1, p, c, me + PLANE)
+
+        @pl.when(z >= x_old)
+        def _():
+            sent(2, x_old, p, c, base + px)
+
+        @pl.when(z >= y_old)
+        def _():
+            sent(3, y_old, p, c, base + py)
+
+        @pl.when(z >= 1)
+        def _():
+            @pl.when(z + 1 < n_z)
+            def _():
+                sent(1, 2, p, c, me + PLANE)
+            sent(4, 1, p, c, base + px)
+            sent(5, 1, p, c, base + py)
+            sent(6, 1, px, c, base + py)
+
+        @pl.when(z >= y_from)
+        def _():
+            sent(7, y_from, py, c, base + px)
+    each(drain)
+
+    @pl.when(me == 0)
+    def _():
+        sink_copy(0, sink, base + px).wait_send()
+
+    @pl.when(me <= 1)
+    def _():
+        sink_copy(1, sink, base + py).wait_send()
+
+    @pl.when(z + 1 < n_z)
+    def _():
+        sink_copy(2, sink, me + PLANE).wait_send()
+
     def finish(t, carry):
         whole = part[t, side].astype(jnp.float32)
         for step in range(1, n_head):
@@ -404,48 +483,6 @@
         return carry
     lax.fori_loop(0, tiles, finish, 0)
 
-    def sent(kind, plane, source, c, target):
-        send(kind, held(plane, source, c), plane, source, c, target).wait_send()
-
-    def drain(c):
-        @pl.when(z + 1 < n_z)
-        def _():
-            sent(0, 1, p, c, me + PLANE)
-
-        @pl.when(z >= x_old)
-        def _():
-            sent(2, x_old, p, c, base + px)
-
-        @pl.when(z >= y_old)
-        def _():
-            sent(3, y_old, p, c, base + py)
-
-        @pl.when(z >= 1)
-        def _():
-            @pl.when(z + 1 < n_z)
-            def _():
-                sent(1, 2, p, c, me + PLANE)
-            sent(4, 1, p, c, base + px)
-            sent(5, 1, p, c, base + py)
-            sent(6, 1, px, c, base + py)
-
-        @pl.when(z >= y_from)
-        def _():
-            sent(7, y_from, py, c, base + px)
-    each(drain)
-
-    @pl.when(me == 0)
-    def _():
-        sink_copy(0, sink, base + px).wait_send()
-
-    @pl.when(me <= 1)
-    def _():
-        sink_copy(1, sink, base + py).wait_send()
-
-    @pl.when(z + 1 < n_z)
-    def _():
-        sink_copy(2, sink, me + PLANE).wait_send()
-
     def gone(t, carry):
         for step in range(1, n_head):
             give(t, step).wait_send()
@@ -460,7 +497,7 @@
     lanes = group * rows
     depth, model = out_weight.shape
     assert (WINDOW - 1) // rows + 1 == 2 * PLANE and n_seq % PLANE == 0
-    tile, wide = min(512, model), min(1024, model)
+    tile, wide = min(1024, model), min(2048, model)
     tiles = model // tile
     share = rows // n_head
     bf16, f32, i32 = jnp.bfloat16, jnp.float32, jnp.int32
@@ -468,8 +505,8 @@
     smem = pl.BlockSpec(memory_space=pltpu.SMEM)
     dma = pltpu.SemaphoreType.DMA
     return pl.pallas_call(
-        functools.partial(kernel, n_seq, n_head, tile, wide, agenda(kv_heads)),
-        out_shape=jax.ShapeDtypeStruct((share, model), bf16),
+        functools.partial(kernel, n_seq, n_head, tile, wide, *agenda(kv_heads)),
+        out_shape=pltpu.VMEM((share, model), bf16),
         in_specs=[smem, smem, smem] + [pl.BlockSpec(memory_space=pl.ANY)] * 4,
         out_specs=vmem,
         scratch_shapes=[

time: 49.3 us -> 45.5 us (0.923)
  Pallas kernels: 46.6 us -> 43.9 us
  local copies, waits for them, and re-layouts: 2.06 us -> 0.88 us
    pallas_call x1, Pallas kernels: 46.6 us -> 43.9 us  [shards(): pl.pallas_call(functools.partial(kernel, n_seq, n_head, tile, wide, *agen...]
    unnamed x1, local copies, waits for them, and re-layouts: 2.06 us -> 0.88 us
where the time goes in v2:
time: 45.5 us; the launch traced here: 44.8 us
  Pallas kernels  43.9 us (96%)
  local copies, waits for them, and re-layouts  0.88 us (2%)
    pallas_call x1, Pallas kernels, shards(): pl.pallas_call(functools.partial(kernel, n_seq, n_head, tile, wide, *agen...  43.9 us

profile of v2, /device:TPU:17, one launch (start us, length us, event | category | flops | bytes accessed | tf_op | source)
XLA Modules:
  0.0 44.8 jit_solution(488924212398437022)
XLA Ops:
  0.0 43.9 %shard_map.73 = bf16[96,4096]{1,0:T(8,128)(2,1)S(1)} custom-call(s32[16]{0:T(128)} %win_ref.1, s32[16]{0:T(128)} %cnt_ref.1, f32[16]{0:T(128)} %bias_ref.1, bf16[768,128]{1,0:T(8,128)(2,1)} %bitcast.4, bf16[768,128]{1,0:T(8,128)(2,1)} %bitcast.5, bf16[3072,128]{1,0:T(8,128)(2,1)} %bitcast.3, bf16[2048,4096]{1,0:T(8,128)(2,1)} %w_hbm.1), custom_call_target="tpu_custom_call" | custom-call | tf_op jit(solution)/shard_map/pallas_call | solution.py:507
  43.9 0.9 %copy.9 = bf16[96,4096]{1,0:T(8,128)(2,1)} copy(bf16[96,4096]{1,0:T(8,128)(2,1)S(1)} %shard_map.73) | data formatting | bytes 1572864

commit v3 on v2

--- a/solution.py
+++ b/solution.py
@@ -18,10 +18,24 @@
 
 KINDS = 8
 PAIRS = KINDS // 2
-PAIR = KINDS
-SINK_EARLY, SINK_MID, SINK_LATE = PAIR + PAIRS, PAIR + PAIRS + 1, PAIR + PAIRS + 2
-CHUNK_US, HOP_US = 2.1, 1.7
-BITS, PER_WORD = 6, 5
+PAIR, LAST, SINK, NOTHING = KINDS, KINDS + PAIRS, KINDS + 2 * PAIRS, KINDS + 2 * PAIRS + 3
+BITS, PER_WORD = 10, 3
+AHEAD = 2
+CHUNK_US, HOP_US = 2.13, 2.0
+BY_Z, BY_X, BY_Y = 1, 2, 4
+ORDERS = {
+    4: (
+        ((1, 2), (2,), (1, 3)),
+        [
+            [0, 8, 1, 4, 2, 16, 5, 24, 9, 17, 6, 20, 13, 14, 3, 10, 21, 25, 12, 15, 28, 27, 11, 29, 26, 7, 18, 22, 30, 19, 23, 31],
+            [0, 20, 1, 4, 12, 13, 2, 22, 24, 8, 23, 21, 14, 6, 3, 9, 25, 16, 10, 17, 7, 26, 15, 5, 28, 29, 27, 11, 18, 19, 31, 30],
+            [0, 1, 4, 8, 24, 26, 2, 5, 12, 25, 28, 29, 27, 3, 13, 9, 7, 6, 16, 30, 14, 20, 31, 21, 10, 11, 15, 18, 17, 22, 19, 23],
+            [0, 24, 1, 21, 22, 25, 4, 26, 2, 23, 20, 27, 5, 8, 3, 30, 12, 13, 28, 14, 7, 6, 15, 16, 10, 29, 18, 11, 31, 9, 17, 19],
+        ],
+        [[0, 3, 1, 2, 5, 7, 6, 4], [0, 5, 6, 3, 2, 1, 7, 4], [0, 6, 2, 1, 3, 7, 5, 4], [3, 7, 0, 5, 1, 6, 2, 4]],
+        ((1, 5, 16), (3, 12, 17), (2, 13, 16), (8, 15, 23)),
+    ),
+}
 
 
 def kinds_of(p):
@@ -30,31 +44,27 @@
     return [(1, p), (2, p), (1, px), (1, py), (1, pd), (2 - 2 * b0, px), (2 - 2 * b1, py), (2 - 2 * b1, pd)]
 
 
-def forwards(z, p, plane, src):
+def forwards(p, plane, src, c, routes):
+    over_z_x, over_z_y, corner_by_x = routes
     b0, b1 = p % 2, p // 2
     px, py = p ^ 1, p ^ 2
-    out = []
+    links = 0
     if (plane, src) == (0, p):
-        out.append(("z", z + 1, p, 1))
-        if b0 == 0:
-            out.append(("x", z, px, 0))
-        if b1 == 0:
-            out.append(("y", z, py, 0))
+        links |= BY_Z | (BY_X if b0 == 0 else 0) | (BY_Y if b1 == 0 else 0)
     if (plane, src) == (1, p):
-        out += [("z", z + 1, p, 2), ("x", z, px, 1), ("y", z, py, 1)]
+        links |= BY_Z | BY_X | BY_Y
     if (plane, src) == (2, p):
-        if b0 == 1:
-            out.append(("x", z, px, 2))
-        if b1 == 1:
-            out.append(("y", z, py, 2))
+        links |= (BY_X if b0 == 1 and c not in over_z_x else 0) | (BY_Y if b1 == 1 and c not in over_z_y else 0)
     if (plane, src) == (1, px):
-        out.append(("y", z, py, 1))
+        links |= (0 if c in corner_by_x else BY_Y) | (BY_Z if b0 == 0 and c in over_z_x else 0)
+    if (plane, src) == (1, py):
+        links |= (BY_X if c in corner_by_x else 0) | (BY_Z if b1 == 0 and c in over_z_y else 0)
     if (plane, src) == (2 - 2 * b1, py):
-        out.append(("x", z, px, plane))
-    return out
-
-
-def arrivals(heads):
+        links |= BY_X
+    return links
+
+
+def arrivals(heads, routes):
     queue, free, landed, tick = [], {}, {}, 0
     for c in range(heads):
         for z in range(3):
@@ -64,8 +74,9 @@
     while queue:
         t, _, z, p, plane, src, c = heapq.heappop(queue)
         landed[z, p, plane, src, c] = t
-        for link, z_to, p_to, plane_to in forwards(z, p, plane, src):
-            if z_to < 3:
+        links = forwards(p, plane, src, c, routes)
+        for link, z_to, p_to, plane_to in ((BY_Z, z + 1, p, plane + 1), (BY_X, z, p ^ 1, plane), (BY_Y, z, p ^ 2, plane)):
+            if links & link and z_to < 3:
                 start = max(t, free.get((z, p, link), 0.0))
                 free[z, p, link] = start + CHUNK_US
                 heapq.heappush(queue, (start + CHUNK_US + HOP_US, tick, z_to, p_to, plane_to, src, c))
@@ -74,28 +85,43 @@
 
 
 def agenda(heads):
-    landed = arrivals(heads)
-    plans, orders = [], []
+    if heads in ORDERS:
+        routes, takes, orders, sinks = ORDERS[heads]
+    else:
+        routes, takes, orders, sinks = ((), (), ()), [], [], ((0, 0, 0),) * PLANE
+        landed = arrivals(heads, routes)
+        for p in range(PLANE):
+            kinds = kinds_of(p)
+            when = {k * heads + c: landed[2, p, *kinds[k], c] for k in range(KINDS) for c in range(heads)}
+            takes.append(sorted(when, key=lambda i: (when[i], i)))
+            orders.append(sorted(range(KINDS), key=lambda k: (sum(when[k * heads + c] for c in range(heads)), k)))
+    plans, finals = [], []
     for p in range(PLANE):
-        kinds = kinds_of(p)
-        when = [[landed[2, p, plane, src, c] for c in range(heads)] for plane, src in kinds]
-        order = sorted(range(KINDS), key=lambda k: (sum(when[k]), k))
-        due = [(when[k][c], k, c) for k in range(KINDS) for c in range(heads)]
-        due += [(11.0, SINK_EARLY, 0), (19.3, SINK_MID, 0), (21.7, SINK_LATE, 0)]
-        for j in range(PAIRS):
-            for c in range(heads):
-                if j < PAIRS - 1 or c < heads - 1:
-                    ready = max(when[k][c] for k in order[2 * j:2 * j + 2])
-                    due.append((max(ready, 21.7) if j == PAIRS - 1 else ready, PAIR + j, c))
-        due.sort(key=lambda e: (e[0], PAIR <= e[1] < SINK_EARLY, e[1], e[2]))
-        plans.append([k * heads + c for _, k, c in due])
-        assert max(plans[-1]) < 1 << BITS
-        orders.append(order)
-    return plans, orders
+        plan, seen = [], set()
+        for i, take in enumerate(takes[p]):
+            for turn in range(3):
+                if sinks[p][turn] == i:
+                    plan.append((SINK + turn, 0, 0))
+            k, c = divmod(take, heads)
+            plan.append((k, c, forwards(p, *kinds_of(p)[k], c, routes)))
+            seen.add(take)
+            for j in range(PAIRS):
+                both = orders[p][2 * j:2 * j + 2]
+                if k in both and all(i * heads + c in seen for i in both):
+                    plan.append((PAIR + j, c, 0))
+        for c in range(heads):
+            i = max(i for i, e in enumerate(plan) if PAIR <= e[0] < LAST and e[1] == c)
+            plan[i] = (plan[i][0] - PAIR + LAST, c, 0)
+        final = max(i for i, e in enumerate(plan) if LAST <= e[0] < SINK)
+        finals.append((plan[final][0] - LAST, plan.pop(final)[1]))
+        assert len(seen) == KINDS * heads
+        plan += [(NOTHING, 0, 0)] * (-len(plan) % PER_WORD)
+        plans.append(plan)
+    return plans, orders, finals
 
 
 def kernel(
-    n_seq, n_head, tile, wide, plans, orders,
+    n_seq, n_head, tile, wide, plans, orders, finals,
     win_ref, cnt_ref, bias_ref, k_hbm, v_hbm, q_hbm, w_hbm, out_ref,
     k_raw, v_raw, q_raw, k_wide, v_wide, q_wide,
     own, kv, sink, qt, low, few, lift, top, norm, acc, att, w, total, part, got,
@@ -143,24 +169,72 @@
     for step in range(1, n_head):
         greet({"head": lax.rem(side + step, n_head)})
 
-    def send(kind, src, plane, source, c, target):
+    def send(link, kind, c, slot, src):
+        way = {BY_Z: 0, BY_X: 1, BY_Y: 2}[link]
+        slot_to = slot + PLANE if link == BY_Z else slot
         return pltpu.make_async_remote_copy(
             src_ref=src,
-            dst_ref=kv.at[plane * PLANE + source, c],
-            send_sem=send_sem.at[kind, c],
-            recv_sem=recv_sem.at[plane * PLANE + source, c],
-            device_id={"seq": target},
+            dst_ref=kv.at[slot_to, c],
+            send_sem=send_sem.at[way, kind, c],
+            recv_sem=recv_sem.at[slot_to, c],
+            device_id={"seq": [me + PLANE, base + px, base + py][way]},
             device_id_type=MESH,
         )
 
-    def landed(plane, source, c):
-        send(0, own.at[c], plane, source, c, me).wait_recv()
+    def own_up(c, act):
+        @pl.when(z + 1 < n_z)
+        def _():
+            act(send(BY_Z, KINDS, c, p, own.at[c]))
+
+    def own_aside(c, act):
+        @pl.when(bit0 == 0)
+        def _():
+            act(send(BY_X, KINDS, c, p, own.at[c]))
+
+        @pl.when(bit1 == 0)
+        def _():
+            act(send(BY_Y, KINDS, c, p, own.at[c]))
+
+    def begin(copy):
+        copy.start()
+
+    def sent(copy):
+        copy.wait_send()
+
+    def send(link, kind, c, slot, src):
+        way = {BY_Z: 0, BY_X: 1, BY_Y: 2}[link]
+        slot_to = slot + PLANE if link == BY_Z else slot
+        return pltpu.make_async_remote_copy(
+            src_ref=src,
+            dst_ref=kv.at[slot_to, c],
+            send_sem=send_sem.at[way, kind, c],
+            recv_sem=recv_sem.at[slot_to, c],
+            device_id={"seq": [me + PLANE, base + px, base + py][way]},
+            device_id_type=MESH,
+        )
+
+    def own_up(c, act):
+        @pl.when(z + 1 < n_z)
+        def _():
+            act(send(BY_Z, KINDS, c, p, own.at[c]))
+
+    def own_aside(c, act):
+        @pl.when(bit0 == 0)
+        def _():
+            act(send(BY_X, KINDS, c, p, own.at[c]))
+
+        @pl.when(bit1 == 0)
+        def _():
+            act(send(BY_Y, KINDS, c, p, own.at[c]))
+
+    def begin(copy):
+        copy.start()
+
+    def sent(copy):
+        copy.wait_send()
 
     def held(plane, source, c):
         return kv.at[plane * PLANE + source, c]
-
-    x_old, y_old = 2 * bit0, 2 * bit1
-    x_from, y_from = 2 - 2 * bit0, 2 - 2 * bit1
 
     def sink_copy(way, source, target):
         return pltpu.make_async_remote_copy(
@@ -181,28 +255,28 @@
             own[c, i] = spread[pl.ds(c, rows, stride=heads_kv), :].astype(jnp.bfloat16)
     pl.semaphore_wait(barrier, n_head + 1 + above + below)
 
+    def sinks_on(source, act):
+        @pl.when(me == 0)
+        def _():
+            act(sink_copy(0, source, base + px))
+
+        @pl.when(me <= 1)
+        def _():
+            act(sink_copy(1, source, base + py))
+
+        @pl.when(z + 1 < n_z)
+        def _():
+            act(sink_copy(2, source, me + PLANE))
+
     @pl.when(me == 0)
     def _():
-        sink_copy(0, first_rows, base + px).start()
-        sink_copy(1, first_rows, base + py).start()
-
-        @pl.when(z + 1 < n_z)
-        def _():
-            sink_copy(2, first_rows, me + PLANE).start()
+        sinks_on(first_rows, begin)
         sink[...] = own[:, :, :SINK_ROWS]
 
     for c in range(heads_kv):
-        @pl.when(z + 1 < n_z)
-        def _():
-            send(0, own.at[c], 1, p, c, me + PLANE).start()
-
-        @pl.when(x_old == 0)
-        def _():
-            send(2, own.at[c], 0, p, c, base + px).start()
-
-        @pl.when(y_old == 0)
-        def _():
-            send(3, own.at[c], 0, p, c, base + py).start()
+        if c < AHEAD:
+            own_up(c, begin)
+        own_aside(c, begin)
 
     def fetch(c):
         part_of = pl.ds(pl.multiple_of(c * depth, depth), depth)
@@ -239,10 +313,11 @@
         keys = [block[0] for block in blocks] + ([sink[c, 0]] if last else [])
         values = [block[1] for block in blocks] + ([sink[c, 1]] if last else [])
         turned = jnp.concatenate(values, axis=0).T
+        turned = jnp.concatenate([turned, jnp.ones((SINK_ROWS, turned.shape[1]), jnp.bfloat16)], axis=0)
         key_row = lax.broadcasted_iota(jnp.int32, (rows, 1), 0)
         scores = [[jnp.dot(k, qt[c, :, cols], preferred_element_type=jnp.float32) for k in keys] for cols in parts]
         olds = [top[c, :, cols] for cols in parts]
-        weights, news, fades, sums = [], [], [], []
+        weights, news, fades = [], [], []
         for pieces, old, cols in zip(scores, olds, parts):
             shown = []
             for s, shard in zip(pieces, shards):
@@ -261,12 +336,11 @@
             weights.append(jnp.concatenate([x.astype(jnp.bfloat16) for x in e], axis=0))
             news.append(new)
             fades.append(jnp.exp2(old - new))
-            sums.append(functools.reduce(jnp.add, [jnp.sum(x, axis=0, keepdims=True) for x in e]))
         adds = [jnp.dot(turned, e, preferred_element_type=jnp.float32) for e in weights]
         mixed = []
-        for new, fade, added, add, cols in zip(news, fades, sums, adds, parts):
-            whole = acc[c, :, cols] * fade + add
-            weight = norm[c, :, cols] * fade + added
+        for new, fade, add, cols in zip(news, fades, adds, parts):
+            whole = acc[c, :, cols] * fade + add[:width]
+            weight = norm[c, :, cols] * fade + add[width:width + 1]
             if last:
                 mixed.append((whole * (1.0 / weight)).T.astype(jnp.bfloat16))
             else:
@@ -294,34 +368,105 @@
             return carry
         lax.fori_loop((z + 1) * PLANE * heads_kv, 3 * PLANE * heads_kv, clear, 0)
 
-    def pass_on():
+    @pl.when((z == 0) & (me > 0))
+    def _():
         sink_copy(0, sink, me).wait_recv()
-
-        @pl.when(me == 1)
-        def _():
-            sink_copy(1, sink, base + py).start()
-
-        @pl.when(z + 1 < n_z)
-        def _():
-            sink_copy(2, sink, me + PLANE).start()
+        sinks_on(sink, begin)
+
+    @pl.when(z == 0)
+    def _():
+        for c in range(AHEAD, heads_kv):
+            own_up(c, begin)
 
     def rows_of(c):
         return pl.ds(pl.multiple_of(c * depth, depth), depth)
 
     def at_position(choices):
-        chosen = jnp.int32(choices[0])
+        chosen = choices[0]
         for q in range(1, PLANE):
-            chosen = jnp.where(p == q, jnp.int32(choices[q]), chosen)
+            chosen = jnp.where(p == q, choices[q], chosen)
         return chosen
 
     def packed(codes, bits):
-        return sum(code << (bits * j) for j, code in enumerate(codes))
-
-    n_words = (len(plans[0]) + PER_WORD - 1) // PER_WORD
+        word = sum(code << (bits * j) for j, code in enumerate(codes))
+        return jnp.int32(word - (1 << 32) if word >> 31 else word)
+
+    def shifted(word, bits):
+        return lax.shift_right_logical(word, bits)
+
+    head_bits = (heads_kv - 1).bit_length()
+    coded = [[((kind << head_bits | c) << 3) | links for kind, c, links in plan] for plan in plans]
     words = [
-        at_position([packed(plan[i * PER_WORD:(i + 1) * PER_WORD], BITS) for plan in plans]) for i in range(n_words)
+        at_position([packed(codes[i:i + PER_WORD], BITS) for codes in coded])
+        for i in range(0, len(plans[0]), PER_WORD)
     ]
-    landing = at_position([packed(order, 3) for order in orders])
+    slots_of = [[plane * PLANE + src for plane, src in kinds_of(q)] for q in range(PLANE)]
+    kind_slots = at_position([packed(slots, 4) for slots in slots_of])
+    pair_slots = at_position([packed([slots[k] for k in order], 4) for slots, order in zip(slots_of, orders)])
+
+    def pair(j, c, last=False):
+        both = shifted(pair_slots, 8 * j)
+        slots = [both & 15, shifted(both, 4) & 15]
+        blocks = [kv.at[slot, c] for slot in slots]
+        shards = [base + (slot & 3) - (slot & 12) for slot in slots]
+        if last:
+            attend(blocks, c, shards, last=True)
+            fetch(c).wait()
+        else:
+            @pl.when(z >= shifted(jnp.minimum(*slots), 2))
+            def _():
+                attend(blocks, c, shards)
+
+    def event(code):
+        links, c, kind = code & 7, shifted(code, 3) & ((1 << head_bits) - 1), shifted(code, 3 + head_bits)
+
+        @pl.when(kind < KINDS)
+        def _():
+            slot = shifted(kind_slots, 4 * kind) & 15
+
+            @pl.when(z >= shifted(slot, 2))
+            def _():
+                block = kv.at[slot, c]
+                send(BY_X, kind, c, slot, block).wait_recv()
+
+                @pl.when(links != 0)
+                def _():
+                    @pl.when(((links & BY_Z) != 0) & (z + 1 < n_z))
+                    def _():
+                        send(BY_Z, kind, c, slot, block).start()
+
+                    @pl.when((links & BY_X) != 0)
+                    def _():
+                        send(BY_X, kind, c, slot, block).start()
+
+                    @pl.when((links & BY_Y) != 0)
+                    def _():
+                        send(BY_Y, kind, c, slot, block).start()
+
+                    @pl.when((kind == 0) & (c + AHEAD < heads_kv))
+                    def _():
+                        own_up(c + AHEAD, begin)
+
+        @pl.when(kind >= KINDS)
+        def _():
+            @pl.when(kind < LAST)
+            def _():
+                pair(kind - PAIR, c)
+
+            @pl.when((kind >= LAST) & (kind < SINK))
+            def _():
+                pair(kind - LAST, c, last=True)
+
+                def project(t, carry):
+                    cols = pl.ds(pl.multiple_of(t * wide, wide), wide)
+                    total[:, cols] += jnp.dot(att[...], w[rows_of(c), cols], preferred_element_type=jnp.float32)
+                    return carry
+                lax.fori_loop(0, model // wide, project, 0)
+
+            @pl.when((kind == SINK + jnp.minimum(z, 3) - 1) & (z > 0))
+            def _():
+                sink_copy(0, sink, me).wait_recv()
+                sinks_on(sink, begin)
 
     def pick(index, choices):
         chosen = choices[-1]
@@ -329,81 +474,16 @@
             chosen = jnp.where(index == i, choices[i], chosen)
         return chosen
 
-    def where_is(kind):
-        return pick(kind, [1, 2, 1, 1, 1, x_from, y_from, y_from]), pick(kind, [p, p, px, py, pd, px, py, pd])
-
-    def pair(j, c, last=False):
-        blocks, shards, nearest = [], [], 2
-        for i in range(2):
-            plane, source = where_is(lax.shift_right_logical(landing, 3 * (2 * j + i)) & 7)
-            blocks.append(held(plane, source, c))
-            shards.append(base - plane * PLANE + source)
-            nearest = jnp.minimum(nearest, plane)
-        if last:
-            attend(blocks, c, shards, last=True)
-            fetch(c).wait()
-        else:
-            @pl.when(z >= nearest)
-            def _():
-                attend(blocks, c, shards)
-
-    def event(i, carry):
-        word = pick(i // PER_WORD, words)
-        code = lax.shift_right_logical(word, BITS * lax.rem(i, PER_WORD)) & ((1 << BITS) - 1)
-        kind, c = code // heads_kv, lax.rem(code, heads_kv)
-        plane, source = where_is(kind)
-
-        @pl.when((kind < KINDS) & (z >= plane))
-        def _():
-            landed(plane, source, c)
-
-            @pl.when(kind == 0)
-            def _():
-                @pl.when(z + 1 < n_z)
-                def _():
-                    send(1, held(1, p, c), 2, p, c, me + PLANE).start()
-                send(4, held(1, p, c), 1, p, c, base + px).start()
-                send(5, held(1, p, c), 1, p, c, base + py).start()
-
-            @pl.when((kind == 1) & (x_old == 2))
-            def _():
-                send(2, held(2, p, c), 2, p, c, base + px).start()
-
-            @pl.when((kind == 1) & (y_old == 2))
-            def _():
-                send(3, held(2, p, c), 2, p, c, base + py).start()
-
-            @pl.when(kind == 2)
-            def _():
-                send(6, held(1, px, c), 1, px, c, base + py).start()
-
-            @pl.when(kind == 6)
-            def _():
-                send(7, held(y_from, py, c), y_from, py, c, base + px).start()
-
-        turn = jnp.where(z <= 1, SINK_EARLY, jnp.where(z == 2, SINK_MID, SINK_LATE))
-
-        @pl.when((kind == turn) & (me > 0))
-        def _():
-            pass_on()
-
-        @pl.when((kind >= PAIR) & (kind < PAIR + PAIRS - 1))
-        def _():
-            pair(kind - PAIR, c)
-
-        @pl.when(kind == PAIR + PAIRS - 1)
-        def _():
-            pair(PAIRS - 1, c, last=True)
-
-            def project(t, carry):
-                cols = pl.ds(pl.multiple_of(t * wide, wide), wide)
-                total[:, cols] += jnp.dot(att[...], w[rows_of(c), cols], preferred_element_type=jnp.float32)
-                return carry
-            lax.fori_loop(0, model // wide, project, 0)
+    def few_events(i, carry):
+        def one(_, word):
+            event(word & ((1 << BITS) - 1))
+            return shifted(word, BITS)
+        lax.fori_loop(0, PER_WORD, one, pick(i, words))
         return carry
-    lax.fori_loop(0, len(plans[0]), event, 0)
-
-    pair(PAIRS - 1, heads_kv - 1, last=True)
+    lax.fori_loop(0, len(words), few_events, 0)
+
+    final = at_position([c for _, c in finals])
+    pair(at_position([j for j, _ in finals]), final, last=True)
     tiles = model // tile
 
     def give(t, step):
@@ -419,7 +499,7 @@
 
     def project(t, carry):
         cols = pl.ds(pl.multiple_of(t * tile, tile), tile)
-        whole = total[:, cols] + jnp.dot(att[...], w[rows_of(heads_kv - 1), cols], preferred_element_type=jnp.float32)
+        whole = total[:, cols] + jnp.dot(att[...], w[rows_of(final), cols], preferred_element_type=jnp.float32)
         for d in range(n_head):
             part[t, d] = whole[d * share:(d + 1) * share].astype(jnp.bfloat16)
 
@@ -432,47 +512,34 @@
     for step in range(1, n_head):
         give(tiles - 1, step).start()
 
-    def sent(kind, plane, source, c, target):
-        send(kind, held(plane, source, c), plane, source, c, target).wait_send()
-
-    def drain(c):
-        @pl.when(z + 1 < n_z)
-        def _():
-            sent(0, 1, p, c, me + PLANE)
-
-        @pl.when(z >= x_old)
-        def _():
-            sent(2, x_old, p, c, base + px)
-
-        @pl.when(z >= y_old)
-        def _():
-            sent(3, y_old, p, c, base + py)
-
-        @pl.when(z >= 1)
-        def _():
-            @pl.when(z + 1 < n_z)
+    def drain(q):
+        for plane in range(3):
+            kinds = [(k, c, links) for k, c, links in plans[q] if k < KINDS and kinds_of(q)[k][0] == plane]
+
+            @pl.when(z >= plane)
             def _():
-                sent(1, 2, p, c, me + PLANE)
-            sent(4, 1, p, c, base + px)
-            sent(5, 1, p, c, base + py)
-            sent(6, 1, px, c, base + py)
-
-        @pl.when(z >= y_from)
-        def _():
-            sent(7, y_from, py, c, base + px)
-    each(drain)
-
-    @pl.when(me == 0)
+                for k, c, links in kinds:
+                    for link in (BY_X, BY_Y):
+                        if links & link:
+                            send(link, k, c, 0, own.at[0]).wait_send()
+
+            @pl.when((z >= plane) & (z + 1 < n_z))
+            def _():
+                for k, c, links in kinds:
+                    if links & BY_Z:
+                        send(BY_Z, k, c, 0, own.at[0]).wait_send()
+
+    for q in range(PLANE):
+        @pl.when(p == q)
+        def _():
+            drain(q)
+    for c in range(heads_kv):
+        own_up(c, sent)
+        own_aside(c, sent)
+
+    @pl.when((z > 0) | (me <= 1) | (n_z > 1))
     def _():
-        sink_copy(0, sink, base + px).wait_send()
-
-    @pl.when(me <= 1)
-    def _():
-        sink_copy(1, sink, base + py).wait_send()
-
-    @pl.when(z + 1 < n_z)
-    def _():
-        sink_copy(2, sink, me + PLANE).wait_send()
+        sinks_on(sink, sent)
 
     def finish(t, carry):
         whole = part[t, side].astype(jnp.float32)
@@ -531,7 +598,7 @@
             pltpu.VMEM((rows, model), f32),
             pltpu.VMEM((tiles, n_head, share, tile), bf16),
             pltpu.VMEM((tiles, n_head - 1, share, tile), bf16),
-            dma((8, kv_heads)),
+            dma((3, KINDS + 1, kv_heads)),
             dma((3 * PLANE, kv_heads)),
             dma((3,)),
             dma,

time: 45.5 us -> 42.7 us (0.938); the launches traced: 44.8 us -> 42.5 us
  Pallas kernels: 43.9 us -> 41.6 us
    pallas_call x1, Pallas kernels: 43.9 us -> 41.6 us  [shards(): pl.pallas_call(functools.partial(kernel, n_seq, n_head, tile, wide, *agen...]
where the time goes in v3:
time: 42.7 us; the launch traced here: 42.5 us
  Pallas kernels  41.6 us (97%)
  local copies, waits for them, and re-layouts  0.88 us (2%)
    pallas_call x1, Pallas kernels, shards(): pl.pallas_call(functools.partial(kernel, n_seq, n_head, tile, wide, *agen...  41.6 us
    unnamed x1, local copies, waits for them, and re-layouts  0.88 us

profile of v3, /device:TPU:17, one launch (start us, length us, event | category | flops | bytes accessed | tf_op | source)
XLA Modules:
  0.0 42.5 jit_solution(15281818201144947153)
XLA Ops:
  0.0 41.6 %shard_map.73 = bf16[96,4096]{1,0:T(8,128)(2,1)S(1)} custom-call(s32[16]{0:T(128)} %win_ref.1, s32[16]{0:T(128)} %cnt_ref.1, f32[16]{0:T(128)} %bias_ref.1, bf16[768,128]{1,0:T(8,128)(2,1)} %bitcast.4, bf16[768,128]{1,0:T(8,128)(2,1)} %bitcast.5, bf16[3072,128]{1,0:T(8,128)(2,1)} %bitcast.3, bf16[2048,4096]{1,0:T(8,128)(2,1)} %w_hbm.1), custom_call_target="tpu_custom_call" | custom-call | tf_op jit(solution)/shard_map/pallas_call | solution.py:574
  41.6 0.9 %copy.9 = bf16[96,4096]{1,0:T(8,128)(2,1)} copy(bf16[96,4096]{1,0:T(8,128)(2,1)S(1)} %shard_map.73) | data formatting | bytes 1572864

commit v4 on v3

--- a/solution.py
+++ b/solution.py
@@ -21,6 +21,7 @@
 PAIR, LAST, SINK, NOTHING = KINDS, KINDS + PAIRS, KINDS + 2 * PAIRS, KINDS + 2 * PAIRS + 3
 BITS, PER_WORD = 10, 3
 AHEAD = 2
+SEND_USES = (1, 0, 2, 3, 0, 0, 2, 0, 0)
 CHUNK_US, HOP_US = 2.13, 2.0
 BY_Z, BY_X, BY_Y = 1, 2, 4
 ORDERS = {
@@ -124,7 +125,7 @@
     n_seq, n_head, tile, wide, plans, orders, finals,
     win_ref, cnt_ref, bias_ref, k_hbm, v_hbm, q_hbm, w_hbm, out_ref,
     k_raw, v_raw, q_raw, k_wide, v_wide, q_wide,
-    own, kv, sink, qt, low, few, lift, top, norm, acc, att, w, total, part, got,
+    own, kv, sink, qt, low, few, lift, top, norm, acc, att, att_for, w, total, part, got,
     send_sem, recv_sem, sink_send, sink_recv, raw_sem, w_sem, part_send, part_recv,
 ):
     me, side = lax.axis_index("seq"), lax.axis_index("head")
@@ -169,14 +170,19 @@
     for step in range(1, n_head):
         greet({"head": lax.rem(side + step, n_head)})
 
+    def use_of(kind):
+        if isinstance(kind, int):
+            return SEND_USES[kind]
+        return lax.shift_right_logical(jnp.int32(sum(use << (2 * k) for k, use in enumerate(SEND_USES))), 2 * kind) & 3
+
     def send(link, kind, c, slot, src):
         way = {BY_Z: 0, BY_X: 1, BY_Y: 2}[link]
         slot_to = slot + PLANE if link == BY_Z else slot
         return pltpu.make_async_remote_copy(
             src_ref=src,
             dst_ref=kv.at[slot_to, c],
-            send_sem=send_sem.at[way, kind, c],
-            recv_sem=recv_sem.at[slot_to, c],
+            send_sem=send_sem.at[way, use_of(kind), c],
+            recv_sem=recv_sem.at[slot_to & (2 * PLANE - 1), c],
             device_id={"seq": [me + PLANE, base + px, base + py][way]},
             device_id_type=MESH,
         )
@@ -200,41 +206,6 @@
 
     def sent(copy):
         copy.wait_send()
-
-    def send(link, kind, c, slot, src):
-        way = {BY_Z: 0, BY_X: 1, BY_Y: 2}[link]
-        slot_to = slot + PLANE if link == BY_Z else slot
-        return pltpu.make_async_remote_copy(
-            src_ref=src,
-            dst_ref=kv.at[slot_to, c],
-            send_sem=send_sem.at[way, kind, c],
-            recv_sem=recv_sem.at[slot_to, c],
-            device_id={"seq": [me + PLANE, base + px, base + py][way]},
-            device_id_type=MESH,
-        )
-
-    def own_up(c, act):
-        @pl.when(z + 1 < n_z)
-        def _():
-            act(send(BY_Z, KINDS, c, p, own.at[c]))
-
-    def own_aside(c, act):
-        @pl.when(bit0 == 0)
-        def _():
-            act(send(BY_X, KINDS, c, p, own.at[c]))
-
-        @pl.when(bit1 == 0)
-        def _():
-            act(send(BY_Y, KINDS, c, p, own.at[c]))
-
-    def begin(copy):
-        copy.start()
-
-    def sent(copy):
-        copy.wait_send()
-
-    def held(plane, source, c):
-        return kv.at[plane * PLANE + source, c]
 
     def sink_copy(way, source, target):
         return pltpu.make_async_remote_copy(
@@ -351,6 +322,9 @@
             mixed = jnp.concatenate(mixed, axis=0)
             for g in range(group):
                 att[:, g * width:(g + 1) * width] = mixed[g * rows:(g + 1) * rows]
+                for d in range(n_head):
+                    start = g * rows + d * share
+                    att_for[d, :, g * width:(g + 1) * width] = mixed[start:start + share]
 
     def each(body):
         def one(c, carry):
@@ -487,21 +461,23 @@
     tiles = model // tile
 
     def give(t, step):
-        target = lax.rem(side + step, n_head)
         return pltpu.make_async_remote_copy(
-            src_ref=part.at[t, target],
+            src_ref=part.at[t, step - 1],
             dst_ref=got.at[t, step - 1],
             send_sem=part_send.at[t, step - 1],
             recv_sem=part_recv.at[t, step - 1],
-            device_id={"head": target},
+            device_id={"head": lax.rem(side + step, n_head)},
             device_id_type=MESH,
         )
 
+    def projected(t, target):
+        cols = pl.ds(pl.multiple_of(t * tile, tile), tile)
+        kept = total[pl.ds(pl.multiple_of(target * share, 8), share), cols]
+        return kept + jnp.dot(att_for[target], w[rows_of(final), cols], preferred_element_type=jnp.float32)
+
     def project(t, carry):
-        cols = pl.ds(pl.multiple_of(t * tile, tile), tile)
-        whole = total[:, cols] + jnp.dot(att[...], w[rows_of(final), cols], preferred_element_type=jnp.float32)
-        for d in range(n_head):
-            part[t, d] = whole[d * share:(d + 1) * share].astype(jnp.bfloat16)
+        for step in range(1, n_head):
+            part[t, step - 1] = projected(t, lax.rem(side + step, n_head)).astype(jnp.bfloat16)
 
         @pl.when(t >= 1)
         def _():
@@ -542,7 +518,7 @@
         sinks_on(sink, sent)
 
     def finish(t, carry):
-        whole = part[t, side].astype(jnp.float32)
+        whole = projected(t, side).astype(jnp.bfloat16).astype(jnp.float32)
         for step in range(1, n_head):
             give(t, step).wait_recv()
             whole = whole + got[t, step - 1].astype(jnp.float32)
@@ -564,7 +540,7 @@
     lanes = group * rows
     depth, model = out_weight.shape
     assert (WINDOW - 1) // rows + 1 == 2 * PLANE and n_seq % PLANE == 0
-    tile, wide = min(1024, model), min(2048, model)
+    tile, wide = min(1024, model), min(4096, model)
     tiles = model // tile
     share = rows // n_head
     bf16, f32, i32 = jnp.bfloat16, jnp.float32, jnp.int32
@@ -594,12 +570,13 @@
             pltpu.VMEM((kv_heads, 1, lanes), f32),
             pltpu.VMEM((kv_heads, width, lanes), f32),
             pltpu.VMEM((rows, group * width), bf16),
+            pltpu.VMEM((n_head, share, group * width), bf16),
             pltpu.VMEM((depth, model), bf16),
             pltpu.VMEM((rows, model), f32),
-            pltpu.VMEM((tiles, n_head, share, tile), bf16),
             pltpu.VMEM((tiles, n_head - 1, share, tile), bf16),
-            dma((3, KINDS + 1, kv_heads)),
-            dma((3 * PLANE, kv_heads)),
+            pltpu.VMEM((tiles, n_head - 1, share, tile), bf16),
+            dma((3, 4, kv_heads)),
+            dma((2 * PLANE, kv_heads)),
             dma((3,)),
             dma,
             dma((3,)),

time: 42.7 us -> 41.5 us (0.972)
  Pallas kernels: 41.6 us -> 40.4 us
    pallas_call x1, Pallas kernels: 41.6 us -> 40.4 us  [shards(): pl.pallas_call(functools.partial(kernel, n_seq, n_head, tile, wide, *agen...]
where the time goes in v4:
time: 41.5 us; the launch traced here: 41.3 us
  Pallas kernels  40.4 us (97%)
  local copies, waits for them, and re-layouts  0.88 us (2%)
    pallas_call x1, Pallas kernels, shards(): pl.pallas_call(functools.partial(kernel, n_seq, n_head, tile, wide, *agen...  40.4 us
    unnamed x1, local copies, waits for them, and re-layouts  0.88 us

profile of v4, /device:TPU:17, one launch (start us, length us, event | category | flops | bytes accessed | tf_op | source)
XLA Modules:
  0.0 41.3 jit_solution(8992619636951203643)
XLA Ops:
  0.0 40.4 %shard_map.73 = bf16[96,4096]{1,0:T(8,128)(2,1)S(1)} custom-call(s32[16]{0:T(128)} %win_ref.1, s32[16]{0:T(128)} %cnt_ref.1, f32[16]{0:T(128)} %bias_ref.1, bf16[768,128]{1,0:T(8,128)(2,1)} %bitcast.4, bf16[768,128]{1,0:T(8,128)(2,1)} %bitcast.5, bf16[3072,128]{1,0:T(8,128)(2,1)} %bitcast.3, bf16[2048,4096]{1,0:T(8,128)(2,1)} %w_hbm.1), custom_call_target="tpu_custom_call" | custom-call | tf_op jit(solution)/shard_map/pallas_call | solution.py:550
  40.5 0.9 %copy.9 = bf16[96,4096]{1,0:T(8,128)(2,1)} copy(bf16[96,4096]{1,0:T(8,128)(2,1)S(1)} %shard_map.73) | data formatting | bytes 1572864

commit v5 on v4

--- a/solution.py
+++ b/solution.py
@@ -26,15 +26,15 @@
 BY_Z, BY_X, BY_Y = 1, 2, 4
 ORDERS = {
     4: (
-        ((1, 2), (2,), (1, 3)),
+        ((0, 3), (2,), ()),
         [
-            [0, 8, 1, 4, 2, 16, 5, 24, 9, 17, 6, 20, 13, 14, 3, 10, 21, 25, 12, 15, 28, 27, 11, 29, 26, 7, 18, 22, 30, 19, 23, 31],
-            [0, 20, 1, 4, 12, 13, 2, 22, 24, 8, 23, 21, 14, 6, 3, 9, 25, 16, 10, 17, 7, 26, 15, 5, 28, 29, 27, 11, 18, 19, 31, 30],
-            [0, 1, 4, 8, 24, 26, 2, 5, 12, 25, 28, 29, 27, 3, 13, 9, 7, 6, 16, 30, 14, 20, 31, 21, 10, 11, 15, 18, 17, 22, 19, 23],
-            [0, 24, 1, 21, 22, 25, 4, 26, 2, 23, 20, 27, 5, 8, 3, 30, 12, 13, 28, 14, 7, 6, 15, 16, 10, 29, 18, 11, 31, 9, 17, 19],
+            [0, 12, 8, 40, 1, 10, 20, 24, 4, 32, 2, 3, 5, 36, 28, 9, 13, 41, 25, 14, 42, 6, 21, 37, 33, 16, 44, 15, 11, 17, 22, 38, 26, 43, 34, 27, 35, 29, 45, 30, 18, 46, 19, 31, 47, 7, 23, 39],
+            [0, 20, 1, 12, 40, 21, 2, 23, 22, 8, 24, 36, 5, 4, 32, 14, 42, 6, 3, 13, 41, 9, 33, 16, 25, 37, 26, 38, 15, 28, 44, 10, 34, 43, 7, 29, 17, 27, 39, 11, 35, 45, 30, 18, 46, 19, 31, 47],
+            [0, 24, 32, 1, 4, 8, 5, 2, 26, 34, 12, 25, 29, 3, 44, 9, 45, 20, 33, 36, 27, 35, 6, 21, 16, 7, 28, 40, 14, 10, 11, 47, 13, 46, 37, 18, 30, 17, 41, 42, 23, 15, 39, 22, 38, 31, 19, 43],
+            [0, 1, 25, 26, 4, 2, 23, 22, 34, 24, 5, 12, 8, 3, 44, 35, 9, 45, 21, 33, 28, 40, 16, 36, 7, 14, 13, 6, 27, 10, 46, 20, 32, 15, 30, 42, 29, 41, 11, 47, 17, 37, 18, 38, 19, 39, 31, 43],
         ],
-        [[0, 3, 1, 2, 5, 7, 6, 4], [0, 5, 6, 3, 2, 1, 7, 4], [0, 6, 2, 1, 3, 7, 5, 4], [3, 7, 0, 5, 1, 6, 2, 4]],
-        ((1, 5, 16), (3, 12, 17), (2, 13, 16), (8, 15, 23)),
+        [[6, 0, 1, 5, 3, 2, 4, 7], [1, 2, 5, 6, 0, 3, 7, 4], [6, 0, 3, 5, 4, 7, 2, 1], [0, 5, 6, 4, 7, 3, 2, 1]],
+        ((1, 5, 19), (3, 17, 28), (4, 17, 27), (5, 16, 32)),
     ),
 }
 
@@ -87,35 +87,38 @@
 
 def agenda(heads):
     if heads in ORDERS:
-        routes, takes, orders, sinks = ORDERS[heads]
+        routes, listed, orders, sinks = ORDERS[heads]
     else:
-        routes, takes, orders, sinks = ((), (), ()), [], [], ((0, 0, 0),) * PLANE
+        routes, listed, orders, sinks = ((), (), ()), [], [], ((0, 0, 0),) * PLANE
         landed = arrivals(heads, routes)
         for p in range(PLANE):
             kinds = kinds_of(p)
             when = {k * heads + c: landed[2, p, *kinds[k], c] for k in range(KINDS) for c in range(heads)}
-            takes.append(sorted(when, key=lambda i: (when[i], i)))
             orders.append(sorted(range(KINDS), key=lambda k: (sum(when[k * heads + c] for c in range(heads)), k)))
+            for j in range(PAIRS):
+                for c in range(heads):
+                    when[(PAIR + j) * heads + c] = max(when[k * heads + c] for k in orders[p][2 * j:2 * j + 2])
+            listed.append(sorted(when, key=lambda i: (when[i], i)))
     plans, finals = [], []
     for p in range(PLANE):
         plan, seen = [], set()
-        for i, take in enumerate(takes[p]):
-            for turn in range(3):
-                if sinks[p][turn] == i:
-                    plan.append((SINK + turn, 0, 0))
-            k, c = divmod(take, heads)
-            plan.append((k, c, forwards(p, *kinds_of(p)[k], c, routes)))
-            seen.add(take)
-            for j in range(PAIRS):
-                both = orders[p][2 * j:2 * j + 2]
-                if k in both and all(i * heads + c in seen for i in both):
-                    plan.append((PAIR + j, c, 0))
+        for i, item in enumerate(listed[p]):
+            plan += [(SINK + turn, 0, 0) for turn in range(3) if sinks[p][turn] == i]
+            k, c = divmod(item, heads)
+            if k < KINDS:
+                plan.append((k, c, forwards(p, *kinds_of(p)[k], c, routes)))
+            else:
+                assert all((i, c) in seen for i in orders[p][2 * (k - PAIR):2 * (k - PAIR) + 2])
+                plan.append((k, c, 0))
+            seen.add((k, c))
+        assert len(seen) == len(listed[p]) == (KINDS + PAIRS) * heads
         for c in range(heads):
             i = max(i for i, e in enumerate(plan) if PAIR <= e[0] < LAST and e[1] == c)
             plan[i] = (plan[i][0] - PAIR + LAST, c, 0)
         final = max(i for i, e in enumerate(plan) if LAST <= e[0] < SINK)
         finals.append((plan[final][0] - LAST, plan.pop(final)[1]))
-        assert len(seen) == KINDS * heads
+        for i in [i for i, e in enumerate(plan) if LAST <= e[0] < SINK][-1:]:
+            plan[i] = plan[i][:2] + (1,)
         plan += [(NOTHING, 0, 0)] * (-len(plan) % PER_WORD)
         plans.append(plan)
     return plans, orders, finals
@@ -125,8 +128,8 @@
     n_seq, n_head, tile, wide, plans, orders, finals,
     win_ref, cnt_ref, bias_ref, k_hbm, v_hbm, q_hbm, w_hbm, out_ref,
     k_raw, v_raw, q_raw, k_wide, v_wide, q_wide,
-    own, kv, sink, qt, low, few, lift, top, norm, acc, att, att_for, w, total, part, got,
-    send_sem, recv_sem, sink_send, sink_recv, raw_sem, w_sem, part_send, part_recv,
+    own, kv, sink, qt, low, few, lift, top, norm, acc, held, faded, att, att_for, w, total, leave, far_att, far_w, far_total,
+    send_sem, recv_sem, sink_send, sink_recv, raw_sem, w_sem, swap_send, swap_recv,
 ):
     me, side = lax.axis_index("seq"), lax.axis_index("head")
     heads_kv, _, rows, width = own.shape
@@ -249,13 +252,23 @@
             own_up(c, begin)
         own_aside(c, begin)
 
+    def at_position(choices):
+        chosen = choices[0]
+        for q in range(1, PLANE):
+            chosen = jnp.where(p == q, choices[q], chosen)
+        return chosen
+
+    def rows_of(c):
+        return pl.ds(pl.multiple_of(c * depth, depth), depth)
+
     def fetch(c):
-        part_of = pl.ds(pl.multiple_of(c * depth, depth), depth)
-        return pltpu.make_async_copy(w_hbm.at[part_of], w.at[part_of], w_sem.at[c])
+        return pltpu.make_async_copy(w_hbm.at[rows_of(c)], w.at[rows_of(c)], w_sem.at[c])
+
+    final = at_position([c for _, c in finals])
 
     loads[2].wait()
     for c in range(heads_kv):
-        fetch(c).start()
+        fetch(lax.rem(final + c, heads_kv)).start()
     q_wide[...] = q_raw[...].astype(jnp.float32)
     column = lax.broadcasted_iota(jnp.int32, (1, lanes), 1)
     for c in range(heads_kv):
@@ -280,14 +293,26 @@
     step = min(256, lanes)
     parts = [slice(n, n + step) for n in range(0, lanes, step)]
 
-    def attend(blocks, c, shards, causal=False, last=False):
+    def upright(values):
+        turned = jnp.concatenate(values, axis=0).T
+        return jnp.concatenate([turned, jnp.ones((SINK_ROWS, turned.shape[1]), jnp.bfloat16)], axis=0)
+
+    def settle(blocks, c):
+        turned = upright([block[1] for block in blocks])
+        adds = [jnp.dot(turned, held[:, cols], preferred_element_type=jnp.float32) for cols in parts]
+        for add, cols in zip(adds, parts):
+            fade = faded[:, cols]
+            acc[c, :, cols] = acc[c, :, cols] * fade + add[:width]
+            norm[c, :, cols] = norm[c, :, cols] * fade + add[width:width + 1]
+
+    def attend(blocks, c, shards, causal=False, last=False, owed=None):
         keys = [block[0] for block in blocks] + ([sink[c, 0]] if last else [])
         values = [block[1] for block in blocks] + ([sink[c, 1]] if last else [])
-        turned = jnp.concatenate(values, axis=0).T
-        turned = jnp.concatenate([turned, jnp.ones((SINK_ROWS, turned.shape[1]), jnp.bfloat16)], axis=0)
         key_row = lax.broadcasted_iota(jnp.int32, (rows, 1), 0)
         scores = [[jnp.dot(k, qt[c, :, cols], preferred_element_type=jnp.float32) for k in keys] for cols in parts]
         olds = [top[c, :, cols] for cols in parts]
+        if owed is not None:
+            settle(*owed)
         weights, news, fades = [], [], []
         for pieces, old, cols in zip(scores, olds, parts):
             shown = []
@@ -307,6 +332,13 @@
             weights.append(jnp.concatenate([x.astype(jnp.bfloat16) for x in e], axis=0))
             news.append(new)
             fades.append(jnp.exp2(old - new))
+        if owed is not None and not last:
+            for new, fade, e, cols in zip(news, fades, weights, parts):
+                top[c, :, cols] = new
+                faded[:, cols] = fade
+                held[:, cols] = e
+            return
+        turned = upright(values)
         adds = [jnp.dot(turned, e, preferred_element_type=jnp.float32) for e in weights]
         mixed = []
         for new, fade, add, cols in zip(news, fades, adds, parts):
@@ -319,6 +351,8 @@
                 norm[c, :, cols] = weight
                 acc[c, :, cols] = whole
         if last:
+            held[...] = jnp.zeros(held.shape, jnp.bfloat16)
+            faded[...] = jnp.ones(faded.shape, jnp.float32)
             mixed = jnp.concatenate(mixed, axis=0)
             for g in range(group):
                 att[:, g * width:(g + 1) * width] = mixed[g * rows:(g + 1) * rows]
@@ -334,6 +368,27 @@
 
     each(lambda c: attend([own.at[c]], c, [me], causal=True))
     total[...] = jnp.zeros(total.shape, jnp.float32)
+    held[...] = jnp.zeros(held.shape, jnp.bfloat16)
+    faded[...] = jnp.ones(faded.shape, jnp.float32)
+    kv[p, 0] = jnp.zeros(own.shape[1:], jnp.bfloat16)
+
+    def swap(what, step):
+        target = lax.rem(side + step, n_head)
+        source, landing = [
+            (w.at[rows_of(final)], far_w), (leave.at[step - 1], far_total), (att_for.at[target], far_att)
+        ][what]
+        return pltpu.make_async_remote_copy(
+            src_ref=source,
+            dst_ref=landing.at[step - 1],
+            send_sem=swap_send.at[what, step - 1],
+            recv_sem=swap_recv.at[what, step - 1],
+            device_id={"head": target},
+            device_id_type=MESH,
+        )
+
+    fetch(final).wait()
+    for step in range(1, n_head):
+        swap(0, step).start()
 
     @pl.when(z < 2)
     def _():
@@ -351,15 +406,6 @@
     def _():
         for c in range(AHEAD, heads_kv):
             own_up(c, begin)
-
-    def rows_of(c):
-        return pl.ds(pl.multiple_of(c * depth, depth), depth)
-
-    def at_position(choices):
-        chosen = choices[0]
-        for q in range(1, PLANE):
-            chosen = jnp.where(p == q, choices[q], chosen)
-        return chosen
 
     def packed(codes, bits):
         word = sum(code << (bits * j) for j, code in enumerate(codes))
@@ -378,20 +424,23 @@
     kind_slots = at_position([packed(slots, 4) for slots in slots_of])
     pair_slots = at_position([packed([slots[k] for k in order], 4) for slots, order in zip(slots_of, orders)])
 
-    def pair(j, c, last=False):
+    def slots_at(j):
         both = shifted(pair_slots, 8 * j)
-        slots = [both & 15, shifted(both, 4) & 15]
+        return both & 15, shifted(both, 4) & 15
+
+    def blocks_of(debt):
+        c = shifted(debt, 8)
+        return [kv.at[debt & 15, c], kv.at[shifted(debt, 4) & 15, c]], c
+
+    def pair(j, c, debt, last=False):
+        slots = slots_at(j)
         blocks = [kv.at[slot, c] for slot in slots]
         shards = [base + (slot & 3) - (slot & 12) for slot in slots]
-        if last:
-            attend(blocks, c, shards, last=True)
-            fetch(c).wait()
-        else:
-            @pl.when(z >= shifted(jnp.minimum(*slots), 2))
-            def _():
-                attend(blocks, c, shards)
-
-    def event(code):
+        attend(blocks, c, shards, last=last, owed=blocks_of(debt))
+
+    no_debt = p | (p << 4)
+
+    def event(code, debt):
         links, c, kind = code & 7, shifted(code, 3) & ((1 << head_bits) - 1), shifted(code, 3 + head_bits)
 
         @pl.when(kind < KINDS)
@@ -421,15 +470,19 @@
                     def _():
                         own_up(c + AHEAD, begin)
 
+        slots = slots_at(kind & (PAIRS - 1))
+        runs = (kind >= PAIR) & (kind < LAST) & (z >= shifted(jnp.minimum(slots[0], slots[1]), 2))
+
         @pl.when(kind >= KINDS)
         def _():
-            @pl.when(kind < LAST)
+            @pl.when(runs)
             def _():
-                pair(kind - PAIR, c)
+                pair(kind - PAIR, c, debt)
 
             @pl.when((kind >= LAST) & (kind < SINK))
             def _():
-                pair(kind - LAST, c, last=True)
+                pair(kind - LAST, c, debt, last=True)
+                fetch(c).wait()
 
                 def project(t, carry):
                     cols = pl.ds(pl.multiple_of(t * wide, wide), wide)
@@ -437,10 +490,20 @@
                     return carry
                 lax.fori_loop(0, model // wide, project, 0)
 
+                @pl.when(links == 1)
+                def _():
+                    for step in range(1, n_head):
+                        target = lax.rem(side + step, n_head)
+                        leave[step - 1] = total[pl.ds(pl.multiple_of(target * share, 8), share)].astype(jnp.bfloat16)
+                        swap(1, step).start()
+
             @pl.when((kind == SINK + jnp.minimum(z, 3) - 1) & (z > 0))
             def _():
                 sink_copy(0, sink, me).wait_recv()
                 sinks_on(sink, begin)
+
+        closes = (kind >= LAST) & (kind < SINK)
+        return jnp.where(runs, slots[0] | (slots[1] << 4) | (c << 8), jnp.where(closes, no_debt, debt))
 
     def pick(index, choices):
         chosen = choices[-1]
@@ -448,45 +511,23 @@
             chosen = jnp.where(index == i, choices[i], chosen)
         return chosen
 
-    def few_events(i, carry):
-        def one(_, word):
-            event(word & ((1 << BITS) - 1))
-            return shifted(word, BITS)
-        lax.fori_loop(0, PER_WORD, one, pick(i, words))
+    def few_events(i, debt):
+        def one(_, carry):
+            word, debt = carry
+            return shifted(word, BITS), event(word & ((1 << BITS) - 1), debt)
+        return lax.fori_loop(0, PER_WORD, one, (pick(i, words), debt))[1]
+    debt = lax.fori_loop(0, len(words), few_events, no_debt)
+
+    pair(at_position([j for j, _ in finals]), final, debt, last=True)
+    for step in range(1, n_head):
+        swap(2, step).start()
+    mine = pl.ds(pl.multiple_of(side * share, 8), share)
+
+    def project(t, carry):
+        cols = pl.ds(pl.multiple_of(t * tile, tile), tile)
+        total[mine, cols] += jnp.dot(att_for[side], w[rows_of(final), cols], preferred_element_type=jnp.float32)
         return carry
-    lax.fori_loop(0, len(words), few_events, 0)
-
-    final = at_position([c for _, c in finals])
-    pair(at_position([j for j, _ in finals]), final, last=True)
-    tiles = model // tile
-
-    def give(t, step):
-        return pltpu.make_async_remote_copy(
-            src_ref=part.at[t, step - 1],
-            dst_ref=got.at[t, step - 1],
-            send_sem=part_send.at[t, step - 1],
-            recv_sem=part_recv.at[t, step - 1],
-            device_id={"head": lax.rem(side + step, n_head)},
-            device_id_type=MESH,
-        )
-
-    def projected(t, target):
-        cols = pl.ds(pl.multiple_of(t * tile, tile), tile)
-        kept = total[pl.ds(pl.multiple_of(target * share, 8), share), cols]
-        return kept + jnp.dot(att_for[target], w[rows_of(final), cols], preferred_element_type=jnp.float32)
-
-    def project(t, carry):
-        for step in range(1, n_head):
-            part[t, step - 1] = projected(t, lax.rem(side + step, n_head)).astype(jnp.bfloat16)
-
-        @pl.when(t >= 1)
-        def _():
-            for step in range(1, n_head):
-                give(t - 1, step).start()
-        return carry
-    lax.fori_loop(0, tiles, project, 0)
-    for step in range(1, n_head):
-        give(tiles - 1, step).start()
+    lax.fori_loop(0, model // tile, project, 0)
 
     def drain(q):
         for plane in range(3):
@@ -517,20 +558,25 @@
     def _():
         sinks_on(sink, sent)
 
+    exchanged = (0, 1, 2) if heads_kv > 1 else (0, 2)
+    for step in range(1, n_head):
+        for what in exchanged:
+            swap(what, step).wait_recv()
+
     def finish(t, carry):
-        whole = projected(t, side).astype(jnp.bfloat16).astype(jnp.float32)
+        cols = pl.ds(pl.multiple_of(t * tile, tile), tile)
+        whole = total[mine, cols].astype(jnp.bfloat16).astype(jnp.float32)
         for step in range(1, n_head):
-            give(t, step).wait_recv()
-            whole = whole + got[t, step - 1].astype(jnp.float32)
-        out_ref[:, pl.ds(pl.multiple_of(t * tile, tile), tile)] = whole.astype(jnp.bfloat16)
+            theirs = jnp.dot(far_att[step - 1], far_w[step - 1, :, cols], preferred_element_type=jnp.float32)
+            if heads_kv > 1:
+                theirs = theirs + far_total[step - 1, :, cols].astype(jnp.float32)
+            whole = whole + theirs.astype(jnp.bfloat16).astype(jnp.float32)
+        out_ref[:, cols] = whole.astype(jnp.bfloat16)
         return carry
-    lax.fori_loop(0, tiles, finish, 0)
-
-    def gone(t, carry):
-        for step in range(1, n_head):
-            give(t, step).wait_send()
-        return carry
-    lax.fori_loop(0, tiles, gone, 0)
+    lax.fori_loop(0, model // tile, finish, 0)
+    for step in range(1, n_head):
+        for what in exchanged:
+            swap(what, step).wait_send()
 
 
 def shards(n_seq, n_head, queries, key_rows, value_rows, windows, sink_counts, sink_bias, out_weight):
@@ -540,8 +586,7 @@
     lanes = group * rows
     depth, model = out_weight.shape
     assert (WINDOW - 1) // rows + 1 == 2 * PLANE and n_seq % PLANE == 0
-    tile, wide = min(1024, model), min(4096, model)
-    tiles = model // tile
+    tile, wide = min(4096, model), min(4096, model)
     share = rows // n_head
     bf16, f32, i32 = jnp.bfloat16, jnp.float32, jnp.int32
     vmem = pl.BlockSpec(memory_space=pltpu.VMEM)
@@ -569,20 +614,24 @@
             pltpu.VMEM((kv_heads, 1, lanes), f32),
             pltpu.VMEM((kv_heads, 1, lanes), f32),
             pltpu.VMEM((kv_heads, width, lanes), f32),
+            pltpu.VMEM((2 * rows, lanes), bf16),
+            pltpu.VMEM((1, lanes), f32),
             pltpu.VMEM((rows, group * width), bf16),
             pltpu.VMEM((n_head, share, group * width), bf16),
             pltpu.VMEM((depth, model), bf16),
             pltpu.VMEM((rows, model), f32),
-            pltpu.VMEM((tiles, n_head - 1, share, tile), bf16),
-            pltpu.VMEM((tiles, n_head - 1, share, tile), bf16),
+            pltpu.VMEM((n_head - 1, share, model), bf16),
+            pltpu.VMEM((n_head - 1, share, group * width), bf16),
+            pltpu.VMEM((n_head - 1, group * width, model), bf16),
+            pltpu.VMEM((n_head - 1, share, model), bf16),
             dma((3, 4, kv_heads)),
             dma((2 * PLANE, kv_heads)),
             dma((3,)),
             dma,
             dma((3,)),
             dma((kv_heads,)),
-            dma((tiles, n_head - 1)),
-            dma((tiles, n_head - 1)),
+            dma((3, n_head - 1)),
+            dma((3, n_head - 1)),
         ],
         compiler_params=pltpu.CompilerParams(
             collective_id=0, has_side_effects=True, vmem_limit_bytes=56 * 1024 * 1024

time: 41.5 us -> 40.1 us (0.966)
  Pallas kernels: 40.4 us -> 39 us
    pallas_call x1, Pallas kernels: 40.4 us -> 39 us  [shards(): pl.pallas_call(functools.partial(kernel, n_seq, n_head, tile, wide, *agen...]
where the time goes in v5:
time: 40.1 us; the launch traced here: 39.9 us
  Pallas kernels  39 us (97%)
  local copies, waits for them, and re-layouts  0.88 us (2%)
    pallas_call x1, Pallas kernels, shards(): pl.pallas_call(functools.partial(kernel, n_seq, n_head, tile, wide, *agen...  39 us
    unnamed x1, local copies, waits for them, and re-layouts  0.88 us

profile of v5, /device:TPU:17, one launch (start us, length us, event | category | flops | bytes accessed | tf_op | source)
XLA Modules:
  0.0 39.9 jit_solution(14791499421443537791)
XLA Ops:
  0.0 39.0 %shard_map.73 = bf16[96,4096]{1,0:T(8,128)(2,1)S(1)} custom-call(s32[16]{0:T(128)} %win_ref.1, s32[16]{0:T(128)} %cnt_ref.1, f32[16]{0:T(128)} %bias_ref.1, bf16[768,128]{1,0:T(8,128)(2,1)} %bitcast.4, bf16[768,128]{1,0:T(8,128)(2,1)} %bitcast.5, bf16[3072,128]{1,0:T(8,128)(2,1)} %bitcast.3, bf16[2048,4096]{1,0:T(8,128)(2,1)} %w_hbm.1), custom_call_target="tpu_custom_call" | custom-call | tf_op jit(solution)/shard_map/pallas_call | solution.py:595
  39.1 0.9 %copy.9 = bf16[96,4096]{1,0:T(8,128)(2,1)} copy(bf16[96,4096]{1,0:T(8,128)(2,1)S(1)} %shard_map.73) | data formatting | bytes 1572864

commit v6 on v5

--- a/solution.py
+++ b/solution.py
@@ -21,20 +21,20 @@
 PAIR, LAST, SINK, NOTHING = KINDS, KINDS + PAIRS, KINDS + 2 * PAIRS, KINDS + 2 * PAIRS + 3
 BITS, PER_WORD = 10, 3
 AHEAD = 2
-SEND_USES = (1, 0, 2, 3, 0, 0, 2, 0, 0)
+SEND_USES = (1, 0, 2, 2, 0, 0, 2, 0, 0)
 CHUNK_US, HOP_US = 2.13, 2.0
 BY_Z, BY_X, BY_Y = 1, 2, 4
 ORDERS = {
     4: (
         ((0, 3), (2,), ()),
         [
-            [0, 12, 8, 40, 1, 10, 20, 24, 4, 32, 2, 3, 5, 36, 28, 9, 13, 41, 25, 14, 42, 6, 21, 37, 33, 16, 44, 15, 11, 17, 22, 38, 26, 43, 34, 27, 35, 29, 45, 30, 18, 46, 19, 31, 47, 7, 23, 39],
-            [0, 20, 1, 12, 40, 21, 2, 23, 22, 8, 24, 36, 5, 4, 32, 14, 42, 6, 3, 13, 41, 9, 33, 16, 25, 37, 26, 38, 15, 28, 44, 10, 34, 43, 7, 29, 17, 27, 39, 11, 35, 45, 30, 18, 46, 19, 31, 47],
-            [0, 24, 32, 1, 4, 8, 5, 2, 26, 34, 12, 25, 29, 3, 44, 9, 45, 20, 33, 36, 27, 35, 6, 21, 16, 7, 28, 40, 14, 10, 11, 47, 13, 46, 37, 18, 30, 17, 41, 42, 23, 15, 39, 22, 38, 31, 19, 43],
-            [0, 1, 25, 26, 4, 2, 23, 22, 34, 24, 5, 12, 8, 3, 44, 35, 9, 45, 21, 33, 28, 40, 16, 36, 7, 14, 13, 6, 27, 10, 46, 20, 32, 15, 30, 42, 29, 41, 11, 47, 17, 37, 18, 38, 19, 39, 31, 43],
+            [0, 8, 12, 40, 1, 10, 20, 9, 24, 32, 2, 13, 3, 5, 4, 36, 28, 41, 25, 33, 14, 42, 6, 21, 37, 16, 44, 17, 15, 11, 43, 22, 38, 26, 34, 27, 35, 29, 45, 30, 18, 46, 19, 31, 47, 7, 23, 39],
+            [0, 20, 1, 12, 23, 2, 24, 36, 21, 22, 5, 33, 8, 40, 4, 32, 14, 6, 34, 3, 13, 16, 25, 37, 26, 38, 9, 41, 28, 44, 10, 42, 15, 7, 35, 17, 27, 39, 11, 43, 29, 45, 30, 18, 46, 19, 31, 47],
+            [0, 24, 32, 1, 4, 8, 44, 5, 2, 26, 34, 12, 25, 33, 29, 3, 9, 45, 20, 36, 16, 27, 35, 6, 7, 28, 40, 21, 10, 46, 14, 11, 47, 13, 37, 30, 17, 41, 18, 42, 23, 15, 39, 22, 38, 31, 19, 43],
+            [0, 24, 1, 4, 21, 25, 26, 2, 23, 22, 5, 12, 40, 8, 28, 44, 3, 9, 14, 45, 13, 32, 42, 16, 41, 6, 27, 7, 10, 46, 20, 36, 15, 43, 30, 34, 29, 33, 11, 47, 17, 37, 18, 38, 19, 39, 31, 35],
         ],
-        [[6, 0, 1, 5, 3, 2, 4, 7], [1, 2, 5, 6, 0, 3, 7, 4], [6, 0, 3, 5, 4, 7, 2, 1], [0, 5, 6, 4, 7, 3, 2, 1]],
-        ((1, 5, 19), (3, 17, 28), (4, 17, 27), (5, 16, 32)),
+        [[6, 0, 1, 5, 3, 2, 7, 4], [1, 0, 5, 6, 3, 2, 7, 4], [6, 0, 3, 5, 4, 7, 2, 1], [7, 6, 5, 4, 0, 3, 2, 1]],
+        ((1, 5, 20), (4, 17, 29), (7, 23, 26), (14, 23, 31)),
     ),
 }
 
@@ -88,6 +88,7 @@
 def agenda(heads):
     if heads in ORDERS:
         routes, listed, orders, sinks = ORDERS[heads]
+        assert not set(routes[0]) & set(routes[1]) and not routes[2]
     else:
         routes, listed, orders, sinks = ((), (), ()), [], [], ((0, 0, 0),) * PLANE
         landed = arrivals(heads, routes)
@@ -126,8 +127,8 @@
 
 def kernel(
     n_seq, n_head, tile, wide, plans, orders, finals,
-    win_ref, cnt_ref, bias_ref, k_hbm, v_hbm, q_hbm, w_hbm, out_ref,
-    k_raw, v_raw, q_raw, k_wide, v_wide, q_wide,
+    win_hbm, cnt_hbm, bias_hbm, k_hbm, v_hbm, q_hbm, w_hbm, out_ref,
+    win_ref, cnt_ref, bias_ref, k_raw, v_raw, q_raw, k_wide, v_wide, q_wide,
     own, kv, sink, qt, low, few, lift, top, norm, acc, held, faded, att, att_for, w, total, leave, far_att, far_w, far_total,
     send_sem, recv_sem, sink_send, sink_recv, raw_sem, w_sem, swap_send, swap_recv,
 ):
@@ -155,7 +156,10 @@
     above, below = (z + 1 < n_z).astype(jnp.int32), (z > 0).astype(jnp.int32)
     loads = [
         pltpu.make_async_copy(source, target, raw_sem.at[i])
-        for i, (source, target) in enumerate(((k_hbm, k_raw), (v_hbm, v_raw), (q_hbm, q_raw)))
+        for i, (source, target) in enumerate((
+            (k_hbm, k_raw), (v_hbm, v_raw), (q_hbm, q_raw),
+            (win_hbm, win_ref), (cnt_hbm, cnt_ref), (bias_hbm, bias_ref),
+        ))
     ]
     for load in loads:
         load.start()
@@ -250,6 +254,10 @@
     for c in range(heads_kv):
         if c < AHEAD:
             own_up(c, begin)
+        if c == AHEAD:
+            @pl.when(z == 0)
+            def _():
+                own_up(c, begin)
         own_aside(c, begin)
 
     def at_position(choices):
@@ -266,7 +274,8 @@
 
     final = at_position([c for _, c in finals])
 
-    loads[2].wait()
+    for load in loads[2:]:
+        load.wait()
     for c in range(heads_kv):
         fetch(lax.rem(final + c, heads_kv)).start()
     q_wide[...] = q_raw[...].astype(jnp.float32)
@@ -404,7 +413,7 @@
 
     @pl.when(z == 0)
     def _():
-        for c in range(AHEAD, heads_kv):
+        for c in range(AHEAD + 1, heads_kv):
             own_up(c, begin)
 
     def packed(codes, bits):
@@ -590,14 +599,16 @@
     share = rows // n_head
     bf16, f32, i32 = jnp.bfloat16, jnp.float32, jnp.int32
     vmem = pl.BlockSpec(memory_space=pltpu.VMEM)
-    smem = pl.BlockSpec(memory_space=pltpu.SMEM)
     dma = pltpu.SemaphoreType.DMA
     return pl.pallas_call(
         functools.partial(kernel, n_seq, n_head, tile, wide, *agenda(kv_heads)),
         out_shape=pltpu.VMEM((share, model), bf16),
-        in_specs=[smem, smem, smem] + [pl.BlockSpec(memory_space=pl.ANY)] * 4,
+        in_specs=[pl.BlockSpec(memory_space=pl.ANY)] * 7,
         out_specs=vmem,
         scratch_shapes=[
+            pltpu.SMEM((heads,), i32),
+            pltpu.SMEM((heads,), i32),
+            pltpu.SMEM((heads,), f32),
             pltpu.VMEM((rows * kv_heads, width), bf16),
             pltpu.VMEM((rows * kv_heads, width), bf16),
             pltpu.VMEM((rows * heads, width), bf16),
@@ -624,11 +635,11 @@
             pltpu.VMEM((n_head - 1, share, group * width), bf16),
             pltpu.VMEM((n_head - 1, group * width, model), bf16),
             pltpu.VMEM((n_head - 1, share, model), bf16),
-            dma((3, 4, kv_heads)),
+            dma((3, 3, kv_heads)),
             dma((2 * PLANE, kv_heads)),
             dma((3,)),
             dma,
-            dma((3,)),
+            dma((6,)),
             dma((kv_heads,)),
             dma((3, n_head - 1)),
             dma((3, n_head - 1)),

time: 40.1 us -> 38.9 us (0.970)
  Pallas kernels: 39 us -> 37.9 us
    pallas_call x1, Pallas kernels: 39 us -> 37.9 us  [shards(): pl.pallas_call(functools.partial(kernel, n_seq, n_head, tile, wide, *agen...]
where the time goes in v6:
time: 38.9 us; the launch traced here: 38.8 us
  Pallas kernels  37.9 us (97%)
  local copies, waits for them, and re-layouts  0.88 us (2%)
    pallas_call x1, Pallas kernels, shards(): pl.pallas_call(functools.partial(kernel, n_seq, n_head, tile, wide, *agen...  37.9 us
    unnamed x1, local copies, waits for them, and re-layouts  0.88 us

profile of v6, /device:TPU:17, one launch (start us, length us, event | category | flops | bytes accessed | tf_op | source)
XLA Modules:
  0.0 38.8 jit_solution(17135675553971406941)
XLA Ops:
  0.0 37.9 %shard_map.73 = bf16[96,4096]{1,0:T(8,128)(2,1)S(1)} custom-call(s32[16]{0:T(128)} %win_hbm.1, s32[16]{0:T(128)} %cnt_hbm.1, f32[16]{0:T(128)} %bias_hbm.1, bf16[768,128]{1,0:T(8,128)(2,1)} %bitcast.4, bf16[768,128]{1,0:T(8,128)(2,1)} %bitcast.5, bf16[3072,128]{1,0:T(8,128)(2,1)} %bitcast.3, bf16[2048,4096]{1,0:T(8,128)(2,1)} %w_hbm.1), custom_call_target="tpu_custom_call" | custom-call | tf_op jit(solution)/shard_map/pallas_call | solution.py:603
  37.9 0.9 %copy.9 = bf16[96,4096]{1,0:T(8,128)(2,1)} copy(bf16[96,4096]{1,0:T(8,128)(2,1)S(1)} %shard_map.73) | data formatting | bytes 1572864

commit v7 on v6

--- a/solution.py
+++ b/solution.py
@@ -28,13 +28,13 @@
     4: (
         ((0, 3), (2,), ()),
         [
-            [0, 8, 12, 40, 1, 10, 20, 9, 24, 32, 2, 13, 3, 5, 4, 36, 28, 41, 25, 33, 14, 42, 6, 21, 37, 16, 44, 17, 15, 11, 43, 22, 38, 26, 34, 27, 35, 29, 45, 30, 18, 46, 19, 31, 47, 7, 23, 39],
-            [0, 20, 1, 12, 23, 2, 24, 36, 21, 22, 5, 33, 8, 40, 4, 32, 14, 6, 34, 3, 13, 16, 25, 37, 26, 38, 9, 41, 28, 44, 10, 42, 15, 7, 35, 17, 27, 39, 11, 43, 29, 45, 30, 18, 46, 19, 31, 47],
-            [0, 24, 32, 1, 4, 8, 44, 5, 2, 26, 34, 12, 25, 33, 29, 3, 9, 45, 20, 36, 16, 27, 35, 6, 7, 28, 40, 21, 10, 46, 14, 11, 47, 13, 37, 30, 17, 41, 18, 42, 23, 15, 39, 22, 38, 31, 19, 43],
-            [0, 24, 1, 4, 21, 25, 26, 2, 23, 22, 5, 12, 40, 8, 28, 44, 3, 9, 14, 45, 13, 32, 42, 16, 41, 6, 27, 7, 10, 46, 20, 36, 15, 43, 30, 34, 29, 33, 11, 47, 17, 37, 18, 38, 19, 39, 31, 35],
+            [0, 12, 32, 8, 9, 1, 24, 2, 10, 20, 36, 13, 33, 5, 41, 4, 40, 21, 28, 25, 37, 14, 34, 3, 6, 16, 44, 15, 35, 11, 42, 17, 22, 26, 38, 27, 29, 45, 30, 18, 46, 19, 31, 47, 7, 43, 23, 39],
+            [0, 1, 20, 12, 23, 21, 2, 22, 24, 36, 5, 8, 4, 33, 40, 13, 14, 6, 34, 3, 32, 9, 28, 16, 25, 37, 26, 38, 41, 44, 10, 42, 17, 15, 7, 35, 29, 27, 39, 11, 43, 45, 30, 18, 46, 19, 31, 47],
+            [24, 0, 32, 1, 4, 8, 2, 44, 5, 26, 34, 12, 25, 9, 29, 20, 3, 45, 36, 33, 6, 27, 35, 16, 21, 28, 7, 40, 10, 14, 46, 17, 11, 47, 13, 37, 18, 30, 41, 42, 23, 15, 39, 22, 38, 31, 19, 43],
+            [0, 1, 25, 26, 4, 2, 23, 22, 38, 24, 5, 12, 32, 8, 3, 9, 45, 21, 37, 44, 28, 7, 14, 16, 40, 13, 33, 20, 34, 6, 27, 39, 10, 30, 46, 15, 29, 36, 35, 11, 47, 17, 41, 18, 42, 19, 31, 43],
         ],
-        [[6, 0, 1, 5, 3, 2, 7, 4], [1, 0, 5, 6, 3, 2, 7, 4], [6, 0, 3, 5, 4, 7, 2, 1], [7, 6, 5, 4, 0, 3, 2, 1]],
-        ((1, 5, 20), (4, 17, 29), (7, 23, 26), (14, 23, 31)),
+        [[3, 0, 6, 5, 1, 2, 4, 7], [1, 0, 5, 6, 2, 3, 7, 4], [6, 0, 3, 5, 4, 7, 2, 1], [3, 0, 5, 6, 7, 4, 2, 1]],
+        ((1, 6, 17), (4, 17, 29), (6, 20, 27), (13, 21, 35)),
     ),
 }
 

time: 38.9 us -> 38.7 us (level)
  no operation moved by 1% of the time
where the time goes in v7:
time: 38.7 us; the launch traced here: 38.5 us
  Pallas kernels  37.6 us (97%)
  local copies, waits for them, and re-layouts  0.88 us (2%)
    pallas_call x1, Pallas kernels, shards(): pl.pallas_call(functools.partial(kernel, n_seq, n_head, tile, wide, *agen...  37.6 us
    unnamed x1, local copies, waits for them, and re-layouts  0.88 us

profile of v7, /device:TPU:17, one launch (start us, length us, event | category | flops | bytes accessed | tf_op | source)
XLA Modules:
  0.0 38.5 jit_solution(4759292448309505604)
XLA Ops:
  0.0 37.6 %shard_map.73 = bf16[96,4096]{1,0:T(8,128)(2,1)S(1)} custom-call(s32[16]{0:T(128)} %win_hbm.1, s32[16]{0:T(128)} %cnt_hbm.1, f32[16]{0:T(128)} %bias_hbm.1, bf16[768,128]{1,0:T(8,128)(2,1)} %bitcast.4, bf16[768,128]{1,0:T(8,128)(2,1)} %bitcast.5, bf16[3072,128]{1,0:T(8,128)(2,1)} %bitcast.3, bf16[2048,4096]{1,0:T(8,128)(2,1)} %w_hbm.1), custom_call_target="tpu_custom_call" | custom-call | tf_op jit(solution)/shard_map/pallas_call | solution.py:603
  37.6 0.9 %copy.9 = bf16[96,4096]{1,0:T(8,128)(2,1)} copy(bf16[96,4096]{1,0:T(8,128)(2,1)S(1)} %shard_map.73) | data formatting | bytes 1572864

commit v8 on v7

--- a/solution.py
+++ b/solution.py
@@ -314,7 +314,7 @@
             acc[c, :, cols] = acc[c, :, cols] * fade + add[:width]
             norm[c, :, cols] = norm[c, :, cols] * fade + add[width:width + 1]
 
-    def attend(blocks, c, shards, causal=False, last=False, owed=None):
+    def attend(blocks, c, shards, causal=False, last=False, owed=None, clear=True):
         keys = [block[0] for block in blocks] + ([sink[c, 0]] if last else [])
         values = [block[1] for block in blocks] + ([sink[c, 1]] if last else [])
         key_row = lax.broadcasted_iota(jnp.int32, (rows, 1), 0)
@@ -360,8 +360,9 @@
                 norm[c, :, cols] = weight
                 acc[c, :, cols] = whole
         if last:
-            held[...] = jnp.zeros(held.shape, jnp.bfloat16)
-            faded[...] = jnp.ones(faded.shape, jnp.float32)
+            if clear:
+                held[...] = jnp.zeros(held.shape, jnp.bfloat16)
+                faded[...] = jnp.ones(faded.shape, jnp.float32)
             mixed = jnp.concatenate(mixed, axis=0)
             for g in range(group):
                 att[:, g * width:(g + 1) * width] = mixed[g * rows:(g + 1) * rows]
@@ -441,11 +442,11 @@
         c = shifted(debt, 8)
         return [kv.at[debt & 15, c], kv.at[shifted(debt, 4) & 15, c]], c
 
-    def pair(j, c, debt, last=False):
+    def pair(j, c, debt, last=False, clear=True):
         slots = slots_at(j)
         blocks = [kv.at[slot, c] for slot in slots]
         shards = [base + (slot & 3) - (slot & 12) for slot in slots]
-        attend(blocks, c, shards, last=last, owed=blocks_of(debt))
+        attend(blocks, c, shards, last=last, owed=blocks_of(debt), clear=clear)
 
     no_debt = p | (p << 4)
 
@@ -527,7 +528,7 @@
         return lax.fori_loop(0, PER_WORD, one, (pick(i, words), debt))[1]
     debt = lax.fori_loop(0, len(words), few_events, no_debt)
 
-    pair(at_position([j for j, _ in finals]), final, debt, last=True)
+    pair(at_position([j for j, _ in finals]), final, debt, last=True, clear=False)
     for step in range(1, n_head):
         swap(2, step).start()
     mine = pl.ds(pl.multiple_of(side * share, 8), share)

time: 38.7 us -> 38.6 us (level)
  no operation moved by 1% of the time
where the time goes in v8:
time: 38.6 us; the launch traced here: 38.4 us
  Pallas kernels  37.5 us (97%)
  local copies, waits for them, and re-layouts  0.88 us (2%)
    pallas_call x1, Pallas kernels, shards(): pl.pallas_call(functools.partial(kernel, n_seq, n_head, tile, wide, *agen...  37.5 us
    unnamed x1, local copies, waits for them, and re-layouts  0.88 us

profile of v8, /device:TPU:17, one launch (start us, length us, event | category | flops | bytes accessed | tf_op | source)
XLA Modules:
  0.0 38.4 jit_solution(3848294236126243251)
XLA Ops:
  0.0 37.5 %shard_map.73 = bf16[96,4096]{1,0:T(8,128)(2,1)S(1)} custom-call(s32[16]{0:T(128)} %win_hbm.1, s32[16]{0:T(128)} %cnt_hbm.1, f32[16]{0:T(128)} %bias_hbm.1, bf16[768,128]{1,0:T(8,128)(2,1)} %bitcast.4, bf16[768,128]{1,0:T(8,128)(2,1)} %bitcast.5, bf16[3072,128]{1,0:T(8,128)(2,1)} %bitcast.3, bf16[2048,4096]{1,0:T(8,128)(2,1)} %w_hbm.1), custom_call_target="tpu_custom_call" | custom-call | tf_op jit(solution)/shard_map/pallas_call | solution.py:604
  37.5 0.9 %copy.9 = bf16[96,4096]{1,0:T(8,128)(2,1)} copy(bf16[96,4096]{1,0:T(8,128)(2,1)S(1)} %shard_map.73) | data formatting | bytes 1572864
